TPU v7x, 32 devices: a whole 2x2x4 slice. The times are simulated.
32 devices in a mesh: tok: 4 (over z), out: 4 (over x, core), grp: 2 (over y).
Axes of the slice: x: 2, y: 2, z: 4, core: 2. Of those that a mesh axis runs over, the one named last changes fastest.
Arguments:
- activations: bfloat16 [1024, 2, 2048], P(('tok', 'grp'), None, 'out'), may hold values from -16 to 16
- out_grads: bfloat16 [1024, 2, 2048], P(('tok', 'grp'), None, 'out'), may hold values from -16 to 16
- weight: bfloat16 [2, 2048, 4096], P(None, 'out'), may hold values from -0.09375 to 0.09375
Outputs:
- update: bfloat16 [4096, 2, 2048], P(('tok', 'grp'), None, 'out')
- input_grad: bfloat16 [1024, 2, 2048], P(('tok', 'grp'), None, 'out')
All inputs are finite; a program needn't handle non-finite values.
Results may differ from a plain program's by a relative error of at most 0.0092.
Values may be sent and summed in bfloat16 or wider, within the bound.
A program may use at most 64 MiB of HBM per device.

v0:
```python
import math

import jax
import jax.numpy as jnp
from jax import lax
from jax.experimental import pallas as pl
from jax.experimental.pallas import tpu as pltpu
from jax.sharding import PartitionSpec as P

POWER = 3


DAMPING = 0.1
HIGH = lax.Precision.HIGHEST


def spread(piece):
    return lax.all_gather(piece, "out", axis=2, tiled=True)


def token_sums(maker, rows):
    return lax.psum_scatter(
        maker(jnp.int32(0), rows * lax.axis_size(("tok", "grp"))),
        ("tok", "grp"),
        scatter_dimension=0,
        tiled=True,
    )


def shared_rows(piece):
    return lax.all_gather(piece, ("tok", "grp"), axis=0, tiled=True)


def shared_total(vector):
    return lax.psum(vector, ("tok", "out", "grp"))


def diagonal_mask(rows, width, row_start, col_start):
    row_ids = row_start + lax.broadcasted_iota(jnp.int32, (rows, 1, width), 0)
    col_ids = col_start + lax.broadcasted_iota(jnp.int32, (rows, 1, width), 2)
    return jnp.where(row_ids == col_ids, 1.0, 0.0).astype(jnp.float32)


def multiply(left, right, gather_columns):
    row_band = spread(left)
    column_band = gather_columns(right)
    return jnp.einsum("rkj,jkc->rkc", row_band, column_band, preferred_element_type=jnp.float32)


def inverse_roots(tile, row_start, col_start, gather_columns, total):
    rows, count, width = tile.shape
    block = width * lax.axis_size("out")
    mask = diagonal_mask(rows, width, row_start, col_start)
    vector = jnp.ones((count, block), jnp.float32)
    image = vector
    for step in range(POWER):
        columns = lax.dynamic_slice_in_dim(vector, col_start, width, 1)
        part = jnp.einsum("rkc,kc->kr", tile, columns, precision=HIGH)
        placed = lax.dynamic_update_slice_in_dim(
            jnp.zeros((count, block), jnp.float32), part, row_start, 1
        )
        image = total(placed)
        if step + 1 < POWER:
            vector = image / jnp.sqrt(jnp.sum(image * image, axis=1, keepdims=True))
    scale = jnp.sum(vector * image, axis=1) / jnp.sum(vector * vector, axis=1)
    start = tile / scale[None, :, None]
    start_low = start.astype(jnp.bfloat16)
    first_low = ((3.0 * mask - start) / 2.0).astype(jnp.bfloat16)
    square_low = multiply(first_low, first_low, gather_columns).astype(jnp.bfloat16)
    moved = multiply(square_low, start_low, gather_columns)
    second_low = ((3.0 * mask - moved) / 2.0).astype(jnp.bfloat16)
    roots = multiply(first_low, second_low, gather_columns) / jnp.sqrt(scale)[None, :, None]
    return roots.astype(jnp.bfloat16)


def local(activations, out_grads, weight):
    tok_dev, blocks, width = activations.shape
    block = width * lax.axis_size("out")
    token_count = tok_dev * lax.axis_size("tok") * lax.axis_size("grp")
    col_start = lax.axis_index("out") * width
    local_sides = jnp.concatenate([activations, out_grads], axis=1)
    whole_sides = spread(local_sides)
    grads_whole = whole_sides[:, blocks:, :]
    weight_rows = weight.reshape(blocks, width, blocks, block)
    input_grad = jnp.einsum(
        "tjq,bcjq->tbc", grads_whole, weight_rows, preferred_element_type=jnp.float32
    ).astype(jnp.bfloat16)
    rows = block // (lax.axis_size("tok") * lax.axis_size("grp"))
    row_start = lax.axis_index(("tok", "grp")) * rows

    def shared_terms(start, span):
        return jnp.einsum(
            "tkr,tkc->rkc", whole_sides, local_sides, preferred_element_type=jnp.float32
        )

    sums = token_sums(shared_terms, rows)
    tile = sums / token_count + DAMPING * diagonal_mask(rows, width, row_start, col_start)
    roots = inverse_roots(tile, row_start, col_start, shared_rows, shared_total)
    bands = shared_rows(roots)
    whitened = jnp.einsum(
        "tkj,jkc->tkc", whole_sides, bands, preferred_element_type=jnp.float32
    ).astype(jnp.bfloat16)
    acts_whole = spread(whitened[:, :blocks, :]).reshape(tok_dev, blocks * block)
    grads_low = whitened[:, blocks:, :]
    owned_acts = lax.all_to_all(acts_whole, ("tok", "grp"), split_axis=1, concat_axis=0, tiled=True)
    update = jnp.einsum(
        "ta,tbc->abc",
        owned_acts,
        lax.all_gather(grads_low, ("tok", "grp"), axis=0, tiled=True),
        preferred_element_type=jnp.float32,
    )
    update = (update / math.sqrt(token_count)).astype(jnp.bfloat16)
    return (update, input_grad)


MESH = pl.DeviceIdType.MESH
HOPS = (0, 1, 3, 2)
CHUNKS = 8
SPLIT = 2
LAG = 3


def greet(peers):
    barrier = pltpu.get_barrier_semaphore()
    for peer in peers:
        pl.semaphore_signal(barrier, inc=1, device_id=peer, device_id_type=MESH)
    pl.semaphore_wait(barrier, len(peers))


def remote(src, dst, send, recv, peer):
    return pltpu.make_async_remote_copy(
        src_ref=src, dst_ref=dst, send_sem=send, recv_sem=recv, device_id=peer, device_id_type=MESH
    )


def held(z):
    return z + 2 - 3 * ((z + 2) // 3) + z // 3


def neighbours():
    z, o, y = lax.axis_index("tok"), lax.axis_index("out"), lax.axis_index("grp")
    ox = lax.rem(o + 2, 4)
    oc = o + 1 - 2 * lax.rem(o, 2)
    at = lambda a, b, c: {"tok": a, "out": b, "grp": c}
    zs = [lax.rem(z + j, 4) for j in range(4)]
    peers = [at(zs[j], o, y) for j in (1, 2, 3)]
    return z, o, y, ox, oc, zs, peers, at(z, o, 1 - y), at(z, ox, y), at(z, oc, y)


def collect_kernel(pieces, sides, send, recv, local):
    z, o, y, ox, oc, zs, z_peers, y_peer, x_peer, c_peer = neighbours()
    width = pieces.shape[2]
    rows = pieces.shape[1] // SPLIT
    sent = []

    def tile(oi, yi, zi, s):
        return sides.at[
            pl.ds(pl.multiple_of(((yi * 4 + zi) * SPLIT + s) * rows, rows), rows),
            pl.ds(pl.multiple_of(oi * width, width), width),
        ]

    def piece(zi, s):
        return pieces.at[held(zi), pl.ds(s * rows, rows), :]

    def push(src, where, peer):
        copy = remote(src, tile(*where), send.at[len(sent)], sem_of(*where), peer)
        copy.start()
        sent.append(copy)

    def sem_of(oi, yi, zi, s):
        return recv.at[(oi * 8 + yi * 4 + zi) * SPLIT + s]

    def arrived(*where):
        ref = tile(*where)
        remote(ref, ref, send.at[0], sem_of(*where), c_peer).wait_recv()
        return ref

    def forward(src, where, peers):
        for peer in peers:
            push(src, where, peer)

    greet(z_peers + [y_peer, x_peer, c_peer])
    order = [(j, s) for j in HOPS for s in range(SPLIT)]
    owns = []
    for s in range(SPLIT):
        for j in (1, 3, 2):
            push(piece(zs[j], s), (o, y, z, s), z_peers[j - 1])
        forward(piece(z, s), (o, y, z, s), (y_peer, x_peer, c_peer))
        owns.append(pltpu.make_async_copy(piece(z, s), tile(o, y, z, s), local.at[s]))
        owns[-1].start()
    for j, s in order[SPLIT:]:
        where = (o, y, zs[j], s)
        forward(arrived(*where), where, (y_peer, x_peer, c_peer))
    for j, s in order:
        where = (o, 1 - y, zs[j], s)
        forward(arrived(*where), where, (x_peer, c_peer) if s % 2 == 0 else (c_peer,))
        where = (ox, y, zs[j], s)
        forward(arrived(*where), where, (y_peer, c_peer) if s % 2 == 1 else (c_peer,))
    for j, s in order:
        where = (ox, 1 - y, zs[j], s)
        forward(arrived(*where), where, (c_peer,))
    oxc = lax.rem(oc + 2, 4)
    for oi in (oc, oxc):
        for yi in (y, 1 - y):
            for j, s in order:
                arrived(oi, yi, zs[j], s)
    for copy in owns:
        copy.wait()
    for copy in sent:
        copy.wait_send()


def collect(pieces):
    _, rows, width = pieces.shape
    sends = (3 + 3 * 4 + 3 * 4 + 4) * SPLIT
    return pl.pallas_call(
        collect_kernel,
        out_shape=jax.ShapeDtypeStruct((rows * 8, width * 4), pieces.dtype),
        in_specs=[pl.BlockSpec(memory_space=pltpu.VMEM)],
        out_specs=pl.BlockSpec(memory_space=pltpu.VMEM),
        scratch_shapes=[
            pltpu.SemaphoreType.DMA((sends,)),
            pltpu.SemaphoreType.DMA((32 * SPLIT,)),
            pltpu.SemaphoreType.DMA((SPLIT,)),
        ],
        compiler_params=pltpu.CompilerParams(collective_id=0, has_side_effects=True),
        name="collect",
    )(pieces)


def deliver_kernel(
    low, pieces, weight, grads, acts, product,
    raw, held_weight, w_sem, r_send, r_recv, g_send, y_send, g_recv, y_recv,
    a_send, a_recv, x_send, x_recv, c_send, c_recv, local,
):
    z, o, y, ox, oc, zs, z_peers, y_peer, x_peer, c_peer = neighbours()
    tokens, part = low.shape
    rows = tokens // CHUNKS
    width = pieces.shape[2]
    block = raw.shape[2]
    strip = width // 2
    is_grad = (z == 0) | (z == 3)
    is_act = jnp.logical_not(is_grad)
    mine = z // 3
    h = o // 2
    goal_z = (z // 2) * 2 + lax.rem(o, 2)
    stays = goal_z == z
    goal = {"tok": goal_z, "out": o, "grp": y}
    near, far = z // 2, 1 - z // 2
    is_hub = lax.rem(o, 2) == lax.rem(z, 2)
    here = is_act & stays
    greet(z_peers + [y_peer, x_peer, c_peer])

    def band(oi):
        return raw.at[:, :, pl.ds(pl.multiple_of(oi * width, width), width)]

    own_raw = pieces.at[2:4]
    raw_local = pltpu.make_async_copy(own_raw, band(o), r_send.at[3])
    raw_x = remote(own_raw, band(o), r_send.at[0], r_recv.at[0], x_peer)
    raw_c = remote(own_raw, band(o), r_send.at[1], r_recv.at[1], c_peer)
    raw_xc = remote(band(ox), band(ox), r_send.at[2], r_recv.at[2], c_peer)
    raw_x.start()
    raw_c.start()
    raw_local.start()

    def span(c):
        return pl.ds(c * rows, rows)

    def piece(c):
        return low.at[span(c), :]

    def half(i):
        return pl.ds(pl.multiple_of(i * part, part), part)

    def g_tile(b, yi, c):
        return grads.at[b, span(c), half(yi)]

    def a_tile(i, c):
        return acts.at[span(c), half(i)]

    def own_grad(c):
        return pltpu.make_async_copy(piece(c), g_tile(mine, y, c), local.at[c])

    def own_act(c):
        return pltpu.make_async_copy(piece(c), a_tile(h, c), local.at[c])

    def to_plane(src, b, c):
        return remote(src, g_tile(b, y, c), g_send.at[b * CHUNKS + c], g_recv.at[b * CHUNKS + c], {"tok": lax.rem(z + 5 - 2 * b, 4), "out": o, "grp": y})

    def y_copy(src, b, c):
        return remote(src, g_tile(b, y, c), y_send.at[b * CHUNKS + c], y_recv.at[b * CHUNKS + c], y_peer)

    def to_hub(c):
        return remote(piece(c), a_tile(h, c), a_send.at[c], a_recv.at[c], goal)

    def over_x(c, i):
        return remote(a_tile(i, c), a_tile(i, c), x_send.at[c], x_recv.at[c], x_peer)

    def over_core(c, i):
        place = i * CHUNKS + c
        return remote(a_tile(i, c), a_tile(i, c), c_send.at[place], c_recv.at[place], c_peer)

    for c in range(CHUNKS):
        for b in range(2):

            @pl.when(z == 3 * b)
            def _():
                to_plane(piece(c), b, c).start()
                y_copy(piece(c), b, c).start()

        @pl.when(is_grad)
        def _():
            own_grad(c).start()

        @pl.when(here)
        def _():
            own_act(c).start()

        @pl.when(is_act & jnp.logical_not(stays))
        def _():
            to_hub(c).start()

    strips = [(b, i) for b in range(2) for i in range(2)]

    def load(n):
        b, i = strips[n]
        place = (b, pl.ds(i * strip, strip), slice(None))
        return pltpu.make_async_copy(weight.at[place], held_weight.at[place], w_sem.at[n])

    for n in range(4):
        load(n).start()

    def multiply(n):
        b, i = strips[n]
        load(n).wait()
        total = jnp.zeros((raw.shape[1], strip), jnp.float32)
        for k in range(2):
            total += lax.dot_general(
                raw[k],
                held_weight[b, pl.ds(i * strip, strip), pl.ds(k * block, block)],
                (((1,), (1,)), ((), ())),
                preferred_element_type=jnp.float32,
            )
        product[b, :, pl.ds(i * strip, strip)] = total.astype(product.dtype)

    def hub_step(c):
        @pl.when(here)
        def _():
            own_act(c).wait()

        @pl.when(is_hub & jnp.logical_not(here))
        def _():
            ref = a_tile(h, c)
            remote(ref, ref, a_send.at[0], a_recv.at[c], c_peer).wait_recv()

        @pl.when(is_hub)
        def _():
            over_x(c, h).start()
            over_core(c, h).start()

    def cross_step(c):
        @pl.when(is_hub)
        def _():
            over_x(c, 1 - h).wait_recv()
            over_core(c, 1 - h).start()

    def take(b, c):
        ref = g_tile(b, y, c)
        remote(ref, ref, g_send.at[0], g_recv.at[b * CHUNKS + c], c_peer).wait_recv()

        @pl.when(is_act)
        def _():
            to_plane(ref, b, c).start()

        y_copy(ref, b, c).start()

    for step in range(CHUNKS + LAG):
        if step < CHUNKS:

            @pl.when(is_act)
            def _():
                take(near, step)

            hub_step(step)
        if step >= LAG:
            take(far, step - LAG)
        if step == 1:
            raw_x.wait_recv()
            raw_xc.start()
        if step == 2:
            raw_c.wait_recv()
            raw_xc.wait()
            raw_local.wait()
        if 3 <= step < 7:
            multiply(step - 3)
    for c in range(CHUNKS):
        cross_step(c)
    for c in range(CHUNKS):
        for b in range(2):
            ref = g_tile(b, 1 - y, c)
            remote(ref, ref, y_send.at[0], y_recv.at[b * CHUNKS + c], c_peer).wait_recv()
            y_copy(g_tile(b, y, c), b, c).wait_send()

            @pl.when(z != 3 - 3 * b)
            def _():
                to_plane(g_tile(b, y, c), b, c).wait_send()

        @pl.when(is_grad)
        def _():
            own_grad(c).wait()

        @pl.when(is_act & jnp.logical_not(stays))
        def _():
            to_hub(c).wait_send()

        for i in range(2):

            @pl.when(is_hub)
            def _():
                over_core(c, i).wait_send()

            @pl.when(jnp.logical_not(is_hub))
            def _():
                over_core(c, i).wait_recv()

        @pl.when(is_hub)
        def _():
            over_x(c, h).wait_send()

    raw_x.wait_send()
    raw_c.wait_send()


def deliver(low, pieces, weight):
    tokens, part = low.shape
    _, rows, width = pieces.shape
    dma = pltpu.SemaphoreType.DMA
    vmem = pl.BlockSpec(memory_space=pltpu.VMEM)
    return pl.pallas_call(
        deliver_kernel,
        out_shape=(
            jax.ShapeDtypeStruct((2, tokens, 2 * part), low.dtype),
            jax.ShapeDtypeStruct((tokens, 2 * part), low.dtype),
            jax.ShapeDtypeStruct((2, rows, width), low.dtype),
        ),
        in_specs=[vmem, vmem, pl.BlockSpec(memory_space=pl.ANY)],
        out_specs=(vmem, vmem, vmem),
        scratch_shapes=[
            pltpu.VMEM((2, rows, 4 * width), low.dtype),
            pltpu.VMEM(weight.shape, weight.dtype),
            dma((4,)),
            dma((4,)),
            dma((3,)),
            dma((2 * CHUNKS,)),
            dma((2 * CHUNKS,)),
            dma((2 * CHUNKS,)),
            dma((2 * CHUNKS,)),
            dma((CHUNKS,)),
            dma((CHUNKS,)),
            dma((CHUNKS,)),
            dma((CHUNKS,)),
            dma((2 * CHUNKS,)),
            dma((2 * CHUNKS,)),
            dma((CHUNKS,)),
        ],
        compiler_params=pltpu.CompilerParams(collective_id=1, has_side_effects=True),
        name="deliver",
    )(low, pieces, weight)


def whiten_kernel(sides, out, gram, low, ray, head, tail, left, right):
    tokens, block = sides.shape
    part = out.shape[1]
    tile = min(512, tokens)
    steps = tokens // tile
    across = (((1,), (1,)), ((), ()))
    ones = jnp.ones((8, block), sides.dtype)
    ray_0 = lax.dot_general(ones, sides[...], across, preferred_element_type=jnp.float32)[0:1]

    def span(i):
        return pl.ds(pl.multiple_of(i * tile, tile), tile)

    def gram_step(i, ray_2):
        product = lax.dot_general(
            sides[span(i), :], sides[...], across, preferred_element_type=jnp.float32
        )
        row_ids = i * tile + lax.broadcasted_iota(jnp.int32, (tile, tokens), 0)
        col_ids = lax.broadcasted_iota(jnp.int32, (tile, tokens), 1)
        product = product / tokens + jnp.where(row_ids == col_ids, DAMPING, 0.0)
        gram[span(i), :] = product
        column = jnp.sum(product * ray_0, axis=1, keepdims=True)
        ray[:, span(i)] = jnp.transpose(jnp.broadcast_to(column, (tile, 128)))[0:8]
        return ray_2 + jnp.sum(product * column, axis=0, keepdims=True)

    ray_2 = lax.fori_loop(0, steps, gram_step, jnp.zeros((1, tokens), jnp.float32))
    ray_1 = ray[0:1, :]

    def pair(a, b):
        return jnp.sum(a * b, axis=1, keepdims=True)

    dots = [
        pair(ray_0, ray_0),
        pair(ray_0, ray_1),
        pair(ray_1, ray_1),
        pair(ray_1, ray_2),
        pair(ray_2, ray_2),
    ]

    def moment(power):
        total = jnp.full((1, 1), DAMPING**power * block, jnp.float32)
        for i in range(power):
            total = total + DAMPING ** (power - 1 - i) * dots[i] / tokens
        return total

    scale = moment(2 * POWER - 1) / moment(2 * POWER - 2)
    inverse = 1.0 / scale
    root = 1.0 / jnp.sqrt(scale)
    z, o, y = lax.axis_index("tok"), lax.axis_index("out"), lax.axis_index("grp")
    act_start = 2 * (lax.rem(o, 2) * 2 + y) + o // 2
    start = jnp.where((z == 0) | (z == 3), 2 * o + y, act_start) * part
    cols = pl.ds(pl.multiple_of(start, part), part)

    @pl.loop(0, steps)
    def _(i):
        low[span(i), :] = (gram[span(i), :] * inverse).astype(low.dtype)
        left[span(i), :] = sides[span(i), cols]

    def apply(i, source):
        return jnp.dot(low[span(i), :], source[...], preferred_element_type=jnp.float32)

    @pl.loop(0, steps)
    def _(i):
        value = sides[span(i), cols].astype(jnp.float32)
        value = 1.5 * value - 0.5 * apply(i, left)
        head[span(i), :] = value
        right[span(i), :] = value.astype(right.dtype)

    @pl.loop(0, steps)
    def _(i):
        value = apply(i, right)
        tail[span(i), :] = value
        left[span(i), :] = value.astype(left.dtype)

    @pl.loop(0, steps)
    def _(i):
        value = 1.5 * tail[span(i), :] - 0.5 * apply(i, left)
        tail[span(i), :] = value
        right[span(i), :] = value.astype(right.dtype)

    @pl.loop(0, steps)
    def _(i):
        value = 1.5 * tail[span(i), :] - 0.5 * apply(i, right)
        out[span(i), :] = ((1.5 * head[span(i), :] - 0.5 * value) * root).astype(out.dtype)


def whiten(sides, part):
    tokens, block = sides.shape
    return pl.pallas_call(
        whiten_kernel,
        out_shape=jax.ShapeDtypeStruct((tokens, part), sides.dtype),
        in_specs=[pl.BlockSpec(memory_space=pltpu.VMEM)],
        out_specs=pl.BlockSpec(memory_space=pltpu.VMEM),
        scratch_shapes=[
            pltpu.VMEM((tokens, tokens), jnp.float32),
            pltpu.VMEM((tokens, tokens), sides.dtype),
            pltpu.VMEM((8, tokens), jnp.float32),
            pltpu.VMEM((tokens, part), jnp.float32),
            pltpu.VMEM((tokens, part), jnp.float32),
            pltpu.VMEM((tokens, part), sides.dtype),
            pltpu.VMEM((tokens, part), sides.dtype),
        ],
        name="whiten",
    )(sides)


def planes(activations, out_grads, weight):
    tok_dev, _, width = activations.shape
    part = width // lax.axis_size("grp")
    token_count = tok_dev * lax.axis_size(("tok", "grp"))
    pieces = jnp.swapaxes(jnp.concatenate([activations, out_grads], axis=1), 0, 1)
    grads_low, acts_low, product = deliver(whiten(collect(pieces), part), pieces, weight)
    update = jnp.einsum("ta,btc->abc", acts_low, grads_low, preferred_element_type=jnp.float32)
    update = (update / math.sqrt(token_count)).astype(jnp.bfloat16)
    input_grad = jnp.swapaxes(product, 0, 1)
    return (update, input_grad)


def solution(mesh):
    in_specs = (
        P(("tok", "grp"), None, "out"),
        P(("tok", "grp"), None, "out"),
        P(None, "out", None),
    )
    out_specs = (P(("tok", "grp"), None, "out"), P(("tok", "grp"), None, "out"))

    def body(activations, out_grads, weight):
        blocks = activations.shape[1]
        tok, grp, out = (mesh.shape[name] for name in ("tok", "grp", "out"))
        fits = (blocks, tok, grp, out) == (2, 4, 2, 4)
        return (planes if fits else local)(activations, out_grads, weight)

    return jax.shard_map(body, mesh=mesh, in_specs=in_specs, out_specs=out_specs, check_vma=False)
```

profile of v0, /device:TPU:0, one launch (start us, length us, event | category | flops | bytes accessed | tf_op | source)
XLA Modules:
  0.0 90.3 jit_solution(602595944704955048)
XLA Ops:
  0.6 1.0 %copy.5 = bf16[128,2,512]{2,0,1:T(8,128)(2,1)S(1)} copy(bf16[128,2,512]{2,1,0:T(2,128)(2,1)} %param.3) | data formatting | bytes 524288 | tf_op args[0]
  1.6 1.0 %copy.6 = bf16[128,2,512]{2,0,1:T(8,128)(2,1)S(1)} copy(bf16[128,2,512]{2,1,0:T(2,128)(2,1)} %param.4) | data formatting | bytes 524288 | tf_op args[1]
  2.6 0.8 maximum_bitcast_fusion.pieces
  3.4 31.3 %collect.1.sides = bf16[1024,2048]{1,0:T(8,128)(2,1)} custom-call(bf16[4,128,512]{2,1,0:T(8,128)(2,1)} %maximum_bitcast_fusion.pieces), custom_call_target="tpu_custom_call" | custom-call | tf_op jit(solution)/shard_map/collect/pallas_call | solution.py:216
  34.7 13.5 %whiten.1.low = bf16[1024,256]{1,0:T(8,128)(2,1)} custom-call(bf16[1024,2048]{1,0:T(8,128)(2,1)} %collect.1.sides), custom_call_target="tpu_custom_call" | custom-call | tf_op jit(solution)/shard_map/whiten/pallas_call | solution.py:558
  48.2 35.9 %deliver.1 = (bf16[2,1024,512]{2,1,0:T(8,128)(2,1)}, bf16[1024,512]{1,0:T(8,128)(2,1)}, bf16[2,128,512]{2,1,0:T(8,128)(2,1)}) custom-call(bf16[1024,256]{1,0:T(8,128)(2,1)} %whiten.1.low, bf16[4,128,512]{2,1,0:T(8,128)(2,1)} %maximum_bitcast_fusion.pieces, bf16[2,512,4096]{2,1,0:T(8,128)(2,1)} %weight.1), custom_call_target="tpu_custom_call" | custom-call | tf_op jit(solution)/shard_map/deliver/pallas_call | solution.py:439
  84.1 3.2 %multiply_convert_fusion = bf16[512,2,512]{2,0,1:T(8,128)(2,1)S(1)} fusion(bf16[2,1024,512]{2,1,0:T(8,128)(2,1)} %get-tuple-element.6, bf16[1024,512]{1,0:T(8,128)(2,1)} %get-tuple-element.5), kind=kOutput, calls=%fused_computation | convolution fusion | flops 1074790400 | bytes 4194304 | tf_op jit(solution)/shard_map/ta,btc->abc/dot_general | solution.py:582
  87.3 0.0 copy-start
  87.3 2.0 %copy.8 = bf16[512,2,512]{2,1,0:T(2,128)(2,1)} copy(bf16[512,2,512]{2,0,1:T(8,128)(2,1)S(1)} %multiply_convert_fusion) | data formatting | bytes 2097152
  89.3 0.0 copy-done
  89.3 1.0 %copy.9 = bf16[128,2,512]{2,1,0:T(2,128)(2,1)} copy(bf16[128,2,512]{2,0,1:T(8,128)(2,1)S(1)} %bitcast.7) | data formatting | bytes 524288
Async XLA Ops:
  87.3 2.1 %copy-start = (bf16[2,128,512]{2,1,0:T(8,128)(2,1)S(1)}, bf16[2,128,512]{2,1,0:T(8,128)(2,1)}, u32[]{:S(2)}) copy-start(bf16[2,128,512]{2,1,0:T(8,128)(2,1)} %get-tuple-element.7) | copy-start | bytes 786436
where the time goes:
time: 92.1 us; the launch traced here: 90.3 us
  Pallas kernels  80.6 us (88%)
  local copies, waits for them, and re-layouts  4.99 us (5%)
  matrix products  3.19 us (3%)
    pallas_call x1, Pallas kernels, deliver(): pl.pallas_call(deliver_kernel, out_shape=(jax.ShapeDtypeStruct((2, tokens...  35.9 us
    pallas_call x1, Pallas kernels, collect(): pl.pallas_call(collect_kernel, out_shape=jax.ShapeDtypeStruct((rows * 8,...  31.3 us
    pallas_call x1, Pallas kernels, whiten(): pl.pallas_call(whiten_kernel, out_shape=jax.ShapeDtypeStruct((tokens, par...  13.5 us
    unnamed x6, local copies, waits for them, and re-layouts  4.99 us
    dot_general x1, matrix products, planes(): jnp.einsum('ta,btc->abc', acts_low, grads_low, preferred_element_type=jnp...  3.19 us

commit v1 on v0

--- a/solution.py
+++ b/solution.py
@@ -114,9 +114,10 @@
 
 
 MESH = pl.DeviceIdType.MESH
-HOPS = (0, 1, 3, 2)
 CHUNKS = 8
-SPLIT = 2
+PARTS = 4
+LATE = 4
+BEHIND = 2
 LAG = 3
 
 
@@ -147,84 +148,246 @@
     return z, o, y, ox, oc, zs, peers, at(z, o, 1 - y), at(z, ox, y), at(z, oc, y)
 
 
-def collect_kernel(pieces, sides, send, recv, local):
+def hops(z):
+    return (z, z + 1 - 2 * lax.rem(z, 2), 2 - z // 2, 3 - 3 * (z // 2))
+
+
+def gather_kernel(
+    pieces, out, sides, low, head, left, right, tail, rays,
+    z_send, send, recv, c_send, c_recv, local,
+):
     z, o, y, ox, oc, zs, z_peers, y_peer, x_peer, c_peer = neighbours()
+    oxc = lax.rem(oc + 2, 4)
     width = pieces.shape[2]
-    rows = pieces.shape[1] // SPLIT
+    rows = pieces.shape[1] // PARTS
+    group = rows * 8
+    tokens, block = sides.shape
+    part = out.shape[1]
+    near = hops(z)
+    across = (((1,), (1,)), ((), ()))
     sent = []
 
+    def columns(oi):
+        return pl.ds(pl.multiple_of(oi * width, width), width)
+
     def tile(oi, yi, zi, s):
-        return sides.at[
-            pl.ds(pl.multiple_of(((yi * 4 + zi) * SPLIT + s) * rows, rows), rows),
-            pl.ds(pl.multiple_of(oi * width, width), width),
-        ]
+        start = pl.multiple_of(((s * 2 + yi) * 4 + zi) * rows, rows)
+        return sides.at[pl.ds(start, rows), columns(oi)]
 
     def piece(zi, s):
         return pieces.at[held(zi), pl.ds(s * rows, rows), :]
+
+    def sem_of(oi, yi, zi, s):
+        return recv.at[((oi // 2) * 8 + yi * 4 + zi) * PARTS + s]
 
     def push(src, where, peer):
         copy = remote(src, tile(*where), send.at[len(sent)], sem_of(*where), peer)
         copy.start()
         sent.append(copy)
 
-    def sem_of(oi, yi, zi, s):
-        return recv.at[(oi * 8 + yi * 4 + zi) * SPLIT + s]
-
     def arrived(*where):
         ref = tile(*where)
         remote(ref, ref, send.at[0], sem_of(*where), c_peer).wait_recv()
         return ref
 
-    def forward(src, where, peers):
-        for peer in peers:
-            push(src, where, peer)
+    def band(oi, s):
+        return sides.at[pl.ds(s * group, group), columns(oi)]
+
+    def over_core(oi, s, place):
+        n = s * 2 + place
+        return remote(band(oi, s), band(oi, s), c_send.at[n], c_recv.at[n], c_peer)
 
     greet(z_peers + [y_peer, x_peer, c_peer])
-    order = [(j, s) for j in HOPS for s in range(SPLIT)]
+    z_sent = []
+    for s in range(PARTS):
+        for j in (3, 2, 1):
+            copy = remote(
+                piece(near[j], s), tile(o, y, z, s), z_send.at[len(z_sent)], sem_of(o, y, z, s),
+                {"tok": near[j], "out": o, "grp": y},
+            )
+            copy.start()
+            z_sent.append(copy)
+        push(piece(z, s), (o, y, z, s), y_peer)
+        push(piece(z, s), (o, y, z, s), x_peer)
     owns = []
-    for s in range(SPLIT):
-        for j in (1, 3, 2):
-            push(piece(zs[j], s), (o, y, z, s), z_peers[j - 1])
-        forward(piece(z, s), (o, y, z, s), (y_peer, x_peer, c_peer))
+    for s in range(PARTS):
         owns.append(pltpu.make_async_copy(piece(z, s), tile(o, y, z, s), local.at[s]))
         owns[-1].start()
-    for j, s in order[SPLIT:]:
-        where = (o, y, zs[j], s)
-        forward(arrived(*where), where, (y_peer, x_peer, c_peer))
-    for j, s in order:
-        where = (o, 1 - y, zs[j], s)
-        forward(arrived(*where), where, (x_peer, c_peer) if s % 2 == 0 else (c_peer,))
-        where = (ox, y, zs[j], s)
-        forward(arrived(*where), where, (y_peer, c_peer) if s % 2 == 1 else (c_peer,))
-    for j, s in order:
-        where = (ox, 1 - y, zs[j], s)
-        forward(arrived(*where), where, (c_peer,))
-    oxc = lax.rem(oc + 2, 4)
-    for oi in (oc, oxc):
-        for yi in (y, 1 - y):
-            for j, s in order:
-                arrived(oi, yi, zs[j], s)
-    for copy in owns:
-        copy.wait()
+
+    ones = jnp.ones((16, block), sides.dtype)
+
+    def gram_group(s):
+        here = pl.ds(s * group, group)
+        sums = lax.dot_general(ones, sides[here, :], across, preferred_element_type=jnp.float32)
+        rays[0:8, here] = sums[0:8]
+
+        def step(i, carry):
+            there = pl.ds(pl.multiple_of(i * group, group), group)
+            product = lax.dot_general(
+                sides[here, :], sides[there, :], across, preferred_element_type=jnp.float32
+            )
+            low[here, there] = (product * (1.0 / tokens)).astype(low.dtype)
+            return carry
+
+        lax.fori_loop(0, s + 1, step, 0)
+
+        def mirror(i, carry):
+            there = pl.ds(pl.multiple_of(i * group, group), group)
+            product = lax.dot_general(
+                sides[there, :], sides[here, :], across, preferred_element_type=jnp.float32
+            )
+            low[there, here] = (product * (1.0 / tokens)).astype(low.dtype)
+            return carry
+
+        if s:
+            lax.fori_loop(0, s, mirror, 0)
+
+    order = [(0, s) for s in range(PARTS)]
+    order += [(j, s) for s in range(PARTS) for j in (1, 2, 3)]
+    last = {s: order.index((3, s)) for s in range(PARTS)}
+    for step in range(len(order) + LATE + BEHIND + 1):
+        if step < len(order) and order[step][0]:
+            j, s = order[step]
+            where = (o, y, near[j], s)
+            ref = arrived(*where)
+            push(ref, where, y_peer)
+            push(ref, where, x_peer)
+        if LATE <= step < LATE + len(order):
+            j, s = order[step - LATE]
+            even = (j + s) % 2 == 0
+            where = (o, 1 - y, near[j], s)
+            ref = arrived(*where)
+            if even:
+                push(ref, where, x_peer)
+            where = (ox, y, near[j], s)
+            ref = arrived(*where)
+            if not even:
+                push(ref, where, y_peer)
+            if step - LATE == last[s]:
+                owns[s].wait()
+                over_core(o, s, 0).start()
+        for s in range(PARTS):
+            if step == last[s] + LATE + BEHIND:
+                for j in range(4):
+                    arrived(ox, 1 - y, near[j], s)
+                over_core(ox, s, 1).start()
+            if step == last[s] + LATE + BEHIND + 1:
+                over_core(oc, s, 0).wait_recv()
+                over_core(oxc, s, 1).wait_recv()
+                gram_group(s)
+
+    def pair(a, b):
+        return jnp.sum(a * b, axis=1, keepdims=True)
+
+    def advance(ray):
+        high = ray.astype(low.dtype)
+        rest = ray - high.astype(jnp.float32)
+        middle = rest.astype(low.dtype)
+        least = (rest - middle.astype(jnp.float32)).astype(low.dtype)
+        zero = jnp.zeros((13, tokens), low.dtype)
+        stack = jnp.concatenate([high, middle, least, zero], axis=0)
+        image = jnp.dot(stack, low[...], preferred_element_type=jnp.float32)
+        return image[0:1] + image[1:2] + image[2:3] + DAMPING * ray
+
+    ray_0 = rays[0:1, :]
+    ray_1 = advance(ray_0)
+    ray_2 = advance(ray_1)
+    dots = [
+        pair(ray_0, ray_0),
+        pair(ray_0, ray_1),
+        pair(ray_1, ray_1),
+        pair(ray_1, ray_2),
+        pair(ray_2, ray_2),
+    ]
+
+    def moment(power):
+        total = jnp.full((1, 1), DAMPING**power * block, jnp.float32)
+        for i in range(power):
+            total = total + DAMPING ** (power - 1 - i) * dots[i] / tokens
+        return total
+
+    scale = moment(2 * POWER - 1) / moment(2 * POWER - 2)
+    inverse = 1.0 / scale
+    root = 1.0 / jnp.sqrt(scale)
+    act_start = 2 * (lax.rem(o, 2) * 2 + y) + o // 2
+    is_grad = (z // 3) + (3 - z) // 3
+    start = (is_grad * (2 * o + y) + (1 - is_grad) * act_start) * part
+    cols = pl.ds(pl.multiple_of(start, part), part)
+    tall = min(512, tokens)
+    steps = tokens // tall
+
+    def span(i):
+        return pl.ds(pl.multiple_of(i * tall, tall), tall)
+
+    def apply(i, source, value):
+        image = jnp.dot(low[span(i), :], source[...], preferred_element_type=jnp.float32)
+        return (image + DAMPING * value) * inverse
+
+    left[...] = sides[:, cols]
+
+    @pl.loop(0, steps)
+    def _(i):
+        value = left[span(i), :].astype(jnp.float32)
+        value = 1.5 * value - 0.5 * apply(i, left, value)
+        head[span(i), :] = value
+        right[span(i), :] = value.astype(right.dtype)
+
+    @pl.loop(0, steps)
+    def _(i):
+        value = apply(i, right, head[span(i), :])
+        tail[span(i), :] = value
+        left[span(i), :] = value.astype(left.dtype)
+
+    @pl.loop(0, steps)
+    def _(i):
+        value = tail[span(i), :]
+        value = 1.5 * value - 0.5 * apply(i, left, value)
+        tail[span(i), :] = value
+        right[span(i), :] = value.astype(right.dtype)
+
+    @pl.loop(0, steps)
+    def _(i):
+        value = tail[span(i), :]
+        value = 1.5 * value - 0.5 * apply(i, right, value)
+        out[span(i), :] = ((1.5 * head[span(i), :] - 0.5 * value) * root).astype(out.dtype)
+
+    for copy in z_sent:
+        copy.wait_send()
     for copy in sent:
         copy.wait_send()
-
-
-def collect(pieces):
+    for s in range(PARTS):
+        over_core(o, s, 0).wait_send()
+        over_core(ox, s, 1).wait_send()
+
+
+def gather(pieces, part):
     _, rows, width = pieces.shape
-    sends = (3 + 3 * 4 + 3 * 4 + 4) * SPLIT
+    tokens, block = rows * 8, width * 4
+    dma = pltpu.SemaphoreType.DMA
+    vmem = pl.BlockSpec(memory_space=pltpu.VMEM)
+    sends = (2 * 4 + 2 * 4) * PARTS
     return pl.pallas_call(
-        collect_kernel,
-        out_shape=jax.ShapeDtypeStruct((rows * 8, width * 4), pieces.dtype),
-        in_specs=[pl.BlockSpec(memory_space=pltpu.VMEM)],
-        out_specs=pl.BlockSpec(memory_space=pltpu.VMEM),
+        gather_kernel,
+        out_shape=jax.ShapeDtypeStruct((tokens, part), pieces.dtype),
+        in_specs=[vmem],
+        out_specs=vmem,
         scratch_shapes=[
-            pltpu.SemaphoreType.DMA((sends,)),
-            pltpu.SemaphoreType.DMA((32 * SPLIT,)),
-            pltpu.SemaphoreType.DMA((SPLIT,)),
+            pltpu.VMEM((tokens, block), pieces.dtype),
+            pltpu.VMEM((tokens, tokens), pieces.dtype),
+            pltpu.VMEM((tokens, part), jnp.float32),
+            pltpu.VMEM((tokens, part), pieces.dtype),
+            pltpu.VMEM((tokens, part), pieces.dtype),
+            pltpu.VMEM((tokens, part), jnp.float32),
+            pltpu.VMEM((8, tokens), jnp.float32),
+            dma((3 * PARTS,)),
+            dma((sends,)),
+            dma((16 * PARTS,)),
+            dma((2 * PARTS,)),
+            dma((2 * PARTS,)),
+            dma((PARTS,)),
         ],
         compiler_params=pltpu.CompilerParams(collective_id=0, has_side_effects=True),
-        name="collect",
+        name="gather",
     )(pieces)
 
 
@@ -468,117 +631,12 @@
     )(low, pieces, weight)
 
 
-def whiten_kernel(sides, out, gram, low, ray, head, tail, left, right):
-    tokens, block = sides.shape
-    part = out.shape[1]
-    tile = min(512, tokens)
-    steps = tokens // tile
-    across = (((1,), (1,)), ((), ()))
-    ones = jnp.ones((8, block), sides.dtype)
-    ray_0 = lax.dot_general(ones, sides[...], across, preferred_element_type=jnp.float32)[0:1]
-
-    def span(i):
-        return pl.ds(pl.multiple_of(i * tile, tile), tile)
-
-    def gram_step(i, ray_2):
-        product = lax.dot_general(
-            sides[span(i), :], sides[...], across, preferred_element_type=jnp.float32
-        )
-        row_ids = i * tile + lax.broadcasted_iota(jnp.int32, (tile, tokens), 0)
-        col_ids = lax.broadcasted_iota(jnp.int32, (tile, tokens), 1)
-        product = product / tokens + jnp.where(row_ids == col_ids, DAMPING, 0.0)
-        gram[span(i), :] = product
-        column = jnp.sum(product * ray_0, axis=1, keepdims=True)
-        ray[:, span(i)] = jnp.transpose(jnp.broadcast_to(column, (tile, 128)))[0:8]
-        return ray_2 + jnp.sum(product * column, axis=0, keepdims=True)
-
-    ray_2 = lax.fori_loop(0, steps, gram_step, jnp.zeros((1, tokens), jnp.float32))
-    ray_1 = ray[0:1, :]
-
-    def pair(a, b):
-        return jnp.sum(a * b, axis=1, keepdims=True)
-
-    dots = [
-        pair(ray_0, ray_0),
-        pair(ray_0, ray_1),
-        pair(ray_1, ray_1),
-        pair(ray_1, ray_2),
-        pair(ray_2, ray_2),
-    ]
-
-    def moment(power):
-        total = jnp.full((1, 1), DAMPING**power * block, jnp.float32)
-        for i in range(power):
-            total = total + DAMPING ** (power - 1 - i) * dots[i] / tokens
-        return total
-
-    scale = moment(2 * POWER - 1) / moment(2 * POWER - 2)
-    inverse = 1.0 / scale
-    root = 1.0 / jnp.sqrt(scale)
-    z, o, y = lax.axis_index("tok"), lax.axis_index("out"), lax.axis_index("grp")
-    act_start = 2 * (lax.rem(o, 2) * 2 + y) + o // 2
-    start = jnp.where((z == 0) | (z == 3), 2 * o + y, act_start) * part
-    cols = pl.ds(pl.multiple_of(start, part), part)
-
-    @pl.loop(0, steps)
-    def _(i):
-        low[span(i), :] = (gram[span(i), :] * inverse).astype(low.dtype)
-        left[span(i), :] = sides[span(i), cols]
-
-    def apply(i, source):
-        return jnp.dot(low[span(i), :], source[...], preferred_element_type=jnp.float32)
-
-    @pl.loop(0, steps)
-    def _(i):
-        value = sides[span(i), cols].astype(jnp.float32)
-        value = 1.5 * value - 0.5 * apply(i, left)
-        head[span(i), :] = value
-        right[span(i), :] = value.astype(right.dtype)
-
-    @pl.loop(0, steps)
-    def _(i):
-        value = apply(i, right)
-        tail[span(i), :] = value
-        left[span(i), :] = value.astype(left.dtype)
-
-    @pl.loop(0, steps)
-    def _(i):
-        value = 1.5 * tail[span(i), :] - 0.5 * apply(i, left)
-        tail[span(i), :] = value
-        right[span(i), :] = value.astype(right.dtype)
-
-    @pl.loop(0, steps)
-    def _(i):
-        value = 1.5 * tail[span(i), :] - 0.5 * apply(i, right)
-        out[span(i), :] = ((1.5 * head[span(i), :] - 0.5 * value) * root).astype(out.dtype)
-
-
-def whiten(sides, part):
-    tokens, block = sides.shape
-    return pl.pallas_call(
-        whiten_kernel,
-        out_shape=jax.ShapeDtypeStruct((tokens, part), sides.dtype),
-        in_specs=[pl.BlockSpec(memory_space=pltpu.VMEM)],
-        out_specs=pl.BlockSpec(memory_space=pltpu.VMEM),
-        scratch_shapes=[
-            pltpu.VMEM((tokens, tokens), jnp.float32),
-            pltpu.VMEM((tokens, tokens), sides.dtype),
-            pltpu.VMEM((8, tokens), jnp.float32),
-            pltpu.VMEM((tokens, part), jnp.float32),
-            pltpu.VMEM((tokens, part), jnp.float32),
-            pltpu.VMEM((tokens, part), sides.dtype),
-            pltpu.VMEM((tokens, part), sides.dtype),
-        ],
-        name="whiten",
-    )(sides)
-
-
 def planes(activations, out_grads, weight):
     tok_dev, _, width = activations.shape
     part = width // lax.axis_size("grp")
     token_count = tok_dev * lax.axis_size(("tok", "grp"))
     pieces = jnp.swapaxes(jnp.concatenate([activations, out_grads], axis=1), 0, 1)
-    grads_low, acts_low, product = deliver(whiten(collect(pieces), part), pieces, weight)
+    grads_low, acts_low, product = deliver(gather(pieces, part), pieces, weight)
     update = jnp.einsum("ta,btc->abc", acts_low, grads_low, preferred_element_type=jnp.float32)
     update = (update / math.sqrt(token_count)).astype(jnp.bfloat16)
     input_grad = jnp.swapaxes(product, 0, 1)

time: 92.1 us -> 87.5 us (0.950)
  the two profiles are of different devices: /device:TPU:0 before, /device:TPU:8 now
where the time goes in v1:
time: 87.5 us; the launch traced here: 87.3 us
  Pallas kernels  77.6 us (89%)
  local copies, waits for them, and re-layouts  4.99 us (6%)
  matrix products  3.19 us (4%)
    pallas_call x1, Pallas kernels, gather(): pl.pallas_call(gather_kernel, out_shape=jax.ShapeDtypeStruct((tokens, par...  41.9 us
    pallas_call x1, Pallas kernels, deliver(): pl.pallas_call(deliver_kernel, out_shape=(jax.ShapeDtypeStruct((2, tokens...  35.7 us
    unnamed x6, local copies, waits for them, and re-layouts  4.99 us
    dot_general x1, matrix products, planes(): jnp.einsum('ta,btc->abc', acts_low, grads_low, preferred_element_type=jnp...  3.19 us

profile of v1, /device:TPU:8, one launch (start us, length us, event | category | flops | bytes accessed | tf_op | source)
XLA Modules:
  0.0 87.3 jit_solution(17605173511687142156)
XLA Ops:
  0.6 1.0 %copy.5 = bf16[128,2,512]{2,0,1:T(8,128)(2,1)S(1)} copy(bf16[128,2,512]{2,1,0:T(2,128)(2,1)} %param.3) | data formatting | bytes 524288 | tf_op args[0]
  1.6 1.0 %copy.6 = bf16[128,2,512]{2,0,1:T(8,128)(2,1)S(1)} copy(bf16[128,2,512]{2,1,0:T(2,128)(2,1)} %param.4) | data formatting | bytes 524288 | tf_op args[1]
  2.6 0.8 maximum_bitcast_fusion.pieces
  3.4 41.9 %gather.1.low = bf16[1024,256]{1,0:T(8,128)(2,1)} custom-call(bf16[4,128,512]{2,1,0:T(8,128)(2,1)} %maximum_bitcast_fusion.pieces), custom_call_target="tpu_custom_call" | custom-call | tf_op jit(solution)/shard_map/gather/pallas_call | solution.py:369
  45.4 35.7 %deliver.1 = (bf16[2,1024,512]{2,1,0:T(8,128)(2,1)}, bf16[1024,512]{1,0:T(8,128)(2,1)}, bf16[2,128,512]{2,1,0:T(8,128)(2,1)}) custom-call(bf16[1024,256]{1,0:T(8,128)(2,1)} %gather.1.low, bf16[4,128,512]{2,1,0:T(8,128)(2,1)} %maximum_bitcast_fusion.pieces, bf16[2,512,4096]{2,1,0:T(8,128)(2,1)} %weight.1), custom_call_target="tpu_custom_call" | custom-call | tf_op jit(solution)/shard_map/deliver/pallas_call | solution.py:602
  81.1 3.2 %multiply_convert_fusion = bf16[512,2,512]{2,0,1:T(8,128)(2,1)S(1)} fusion(bf16[2,1024,512]{2,1,0:T(8,128)(2,1)} %get-tuple-element.6, bf16[1024,512]{1,0:T(8,128)(2,1)} %get-tuple-element.5), kind=kOutput, calls=%fused_computation | convolution fusion | flops 1074790400 | bytes 4194304 | tf_op jit(solution)/shard_map/ta,btc->abc/dot_general | solution.py:640
  84.2 0.0 copy-start
  84.3 2.0 %copy.8 = bf16[512,2,512]{2,1,0:T(2,128)(2,1)} copy(bf16[512,2,512]{2,0,1:T(8,128)(2,1)S(1)} %multiply_convert_fusion) | data formatting | bytes 2097152
  86.3 0.0 copy-done
  86.3 1.0 %copy.9 = bf16[128,2,512]{2,1,0:T(2,128)(2,1)} copy(bf16[128,2,512]{2,0,1:T(8,128)(2,1)S(1)} %bitcast.7) | data formatting | bytes 524288
Async XLA Ops:
  84.2 2.1 %copy-start = (bf16[2,128,512]{2,1,0:T(8,128)(2,1)S(1)}, bf16[2,128,512]{2,1,0:T(8,128)(2,1)}, u32[]{:S(2)}) copy-start(bf16[2,128,512]{2,1,0:T(8,128)(2,1)} %get-tuple-element.7) | copy-start | bytes 786436

commit v2 on v1

--- a/solution.py
+++ b/solution.py
@@ -116,8 +116,16 @@
 MESH = pl.DeviceIdType.MESH
 CHUNKS = 8
 PARTS = 4
-LATE = 4
-BEHIND = 2
+PLAN = (
+    ("y", 0, 0), ("x", 0, 0), ("y", 0, 1), ("x", 0, 1), ("z", 1, 0), ("y", 0, 2), ("x", 0, 2),
+    ("z", 2, 0), ("y", 0, 3), ("x", 0, 3), ("z", 3, 0), ("z", 1, 1), ("z", 2, 1), ("y", 1, 0),
+    ("y", 2, 0), ("x", 1, 0), ("z", 1, 2), ("z", 3, 1), ("x", 2, 0), ("z", 2, 2), ("x", 1, 1),
+    ("y", 1, 1), ("x", 3, 0), ("z", 1, 3), ("y", 3, 0), ("c", 0, 0), ("z", 3, 2), ("x", 2, 1),
+    ("x", 1, 2), ("y", 1, 2), ("y", 2, 1), ("z", 2, 3), ("y", 3, 1), ("c", 0, 1), ("z", 3, 3),
+    ("x", 3, 1), ("y", 2, 2), ("x", 2, 2), ("x", 1, 3), ("d", 0, 0), ("x", 3, 2), ("y", 1, 3),
+    ("y", 3, 2), ("c", 0, 2), ("x", 2, 3), ("d", 0, 1), ("y", 2, 3), ("x", 3, 3), ("y", 3, 3),
+    ("c", 0, 3), ("d", 0, 2), ("d", 0, 3),
+)
 LAG = 3
 
 
@@ -197,7 +205,8 @@
         n = s * 2 + place
         return remote(band(oi, s), band(oi, s), c_send.at[n], c_recv.at[n], c_peer)
 
-    greet(z_peers + [y_peer, x_peer, c_peer])
+    d_peer = {"tok": z, "out": ox, "grp": 1 - y}
+    greet(z_peers + [y_peer, x_peer, c_peer, d_peer])
     z_sent = []
     for s in range(PARTS):
         for j in (3, 2, 1):
@@ -216,65 +225,63 @@
 
     ones = jnp.ones((16, block), sides.dtype)
 
-    def gram_group(s):
-        here = pl.ds(s * group, group)
+    def rows_of(s):
+        return pl.ds(s * group, group)
+
+    def gram_group(s, known):
+        here = rows_of(s)
         sums = lax.dot_general(ones, sides[here, :], across, preferred_element_type=jnp.float32)
         rays[0:8, here] = sums[0:8]
-
-        def step(i, carry):
-            there = pl.ds(pl.multiple_of(i * group, group), group)
-            product = lax.dot_general(
-                sides[here, :], sides[there, :], across, preferred_element_type=jnp.float32
-            )
-            low[here, there] = (product * (1.0 / tokens)).astype(low.dtype)
-            return carry
-
-        lax.fori_loop(0, s + 1, step, 0)
-
-        def mirror(i, carry):
-            there = pl.ds(pl.multiple_of(i * group, group), group)
+        for i in known + [s]:
+            there = rows_of(i)
             product = lax.dot_general(
                 sides[there, :], sides[here, :], across, preferred_element_type=jnp.float32
             )
-            low[there, here] = (product * (1.0 / tokens)).astype(low.dtype)
-            return carry
-
-        if s:
-            lax.fori_loop(0, s, mirror, 0)
-
-    order = [(0, s) for s in range(PARTS)]
-    order += [(j, s) for s in range(PARTS) for j in (1, 2, 3)]
-    last = {s: order.index((3, s)) for s in range(PARTS)}
-    for step in range(len(order) + LATE + BEHIND + 1):
-        if step < len(order) and order[step][0]:
-            j, s = order[step]
+            product = product * (1.0 / tokens)
+            low[there, here] = product.astype(low.dtype)
+            if i != s:
+                low[here, there] = jnp.transpose(product).astype(low.dtype)
+
+    def straight(j, s):
+        return j == 3 and s == PARTS - 1
+
+    def finish(s):
+        over_core(oc, s, 0).wait_recv()
+        over_core(oxc, s, 1).wait_recv()
+        gram_group(s, known)
+        known.append(s)
+
+    known = []
+    waiting = []
+    for kind, j, s in PLAN:
+        if kind == "z":
             where = (o, y, near[j], s)
             ref = arrived(*where)
             push(ref, where, y_peer)
             push(ref, where, x_peer)
-        if LATE <= step < LATE + len(order):
-            j, s = order[step - LATE]
-            even = (j + s) % 2 == 0
+            if straight(j, s):
+                push(ref, where, d_peer)
+        elif kind == "y":
             where = (o, 1 - y, near[j], s)
             ref = arrived(*where)
-            if even:
+            if (j + s) % 2 == 0 and not straight(j, s):
                 push(ref, where, x_peer)
+        elif kind == "x":
             where = (ox, y, near[j], s)
             ref = arrived(*where)
-            if not even:
+            if (j + s) % 2 == 1 and not straight(j, s):
                 push(ref, where, y_peer)
-            if step - LATE == last[s]:
-                owns[s].wait()
-                over_core(o, s, 0).start()
-        for s in range(PARTS):
-            if step == last[s] + LATE + BEHIND:
-                for j in range(4):
-                    arrived(ox, 1 - y, near[j], s)
-                over_core(ox, s, 1).start()
-            if step == last[s] + LATE + BEHIND + 1:
-                over_core(oc, s, 0).wait_recv()
-                over_core(oxc, s, 1).wait_recv()
-                gram_group(s)
+        elif kind == "c":
+            owns[s].wait()
+            over_core(o, s, 0).start()
+        else:
+            for i in range(4):
+                arrived(ox, 1 - y, near[i], s)
+            over_core(ox, s, 1).start()
+            if waiting:
+                finish(waiting.pop())
+            waiting.append(s)
+    finish(waiting.pop())
 
     def pair(a, b):
         return jnp.sum(a * b, axis=1, keepdims=True)

time: 87.5 us -> 81.8 us (0.935)
  Pallas kernels: 77.6 us -> 71.8 us
    pallas_call x1, Pallas kernels: 41.9 us -> 36.6 us  [gather(): pl.pallas_call(gather_kernel, out_shape=jax.ShapeDtypeStruct((tokens, par...]
where the time goes in v2:
time: 81.8 us; the launch traced here: 81.5 us
  Pallas kernels  71.8 us (88%)
  local copies, waits for them, and re-layouts  4.99 us (6%)
  matrix products  3.19 us (4%)
  other arithmetic  0.84 us (1%)
    pallas_call x1, Pallas kernels, gather(): pl.pallas_call(gather_kernel, out_shape=jax.ShapeDtypeStruct((tokens, par...  36.6 us
    pallas_call x1, Pallas kernels, deliver(): pl.pallas_call(deliver_kernel, out_shape=(jax.ShapeDtypeStruct((2, tokens...  35.2 us
    unnamed x6, local copies, waits for them, and re-layouts  4.99 us
    dot_general x1, matrix products, planes(): jnp.einsum('ta,btc->abc', acts_low, grads_low, preferred_element_type=jnp...  3.19 us

profile of v2, /device:TPU:8, one launch (start us, length us, event | category | flops | bytes accessed | tf_op | source)
XLA Modules:
  0.0 81.5 jit_solution(7273149099247093466)
XLA Ops:
  0.6 1.0 %copy.5 = bf16[128,2,512]{2,0,1:T(8,128)(2,1)S(1)} copy(bf16[128,2,512]{2,1,0:T(2,128)(2,1)} %param.3) | data formatting | bytes 524288 | tf_op args[0]
  1.6 1.0 %copy.6 = bf16[128,2,512]{2,0,1:T(8,128)(2,1)S(1)} copy(bf16[128,2,512]{2,1,0:T(2,128)(2,1)} %param.4) | data formatting | bytes 524288 | tf_op args[1]
  2.6 0.8 %maximum_bitcast_fusion.pieces = bf16[4,128,512]{2,1,0:T(8,128)(2,1)} fusion(bf16[128,2,512]{2,0,1:T(8,128)(2,1)S(1)} %copy.6, bf16[128,2,512]{2,0,1:T(8,128)(2,1)S(1)} %copy.5), kind=kLoop, calls=%fused_computation.2 | loop fusion | flops 262144 | bytes 1048576 | tf_op jit(solution)/shard_map/transpose | solution.py:645
  3.4 36.6 %gather.1.low = bf16[1024,256]{1,0:T(8,128)(2,1)} custom-call(bf16[4,128,512]{2,1,0:T(8,128)(2,1)} %maximum_bitcast_fusion.pieces), custom_call_target="tpu_custom_call" | custom-call | tf_op jit(solution)/shard_map/gather/pallas_call | solution.py:376
  40.1 35.2 %deliver.1 = (bf16[2,1024,512]{2,1,0:T(8,128)(2,1)}, bf16[1024,512]{1,0:T(8,128)(2,1)}, bf16[2,128,512]{2,1,0:T(8,128)(2,1)}) custom-call(bf16[1024,256]{1,0:T(8,128)(2,1)} %gather.1.low, bf16[4,128,512]{2,1,0:T(8,128)(2,1)} %maximum_bitcast_fusion.pieces, bf16[2,512,4096]{2,1,0:T(8,128)(2,1)} %weight.1), custom_call_target="tpu_custom_call" | custom-call | tf_op jit(solution)/shard_map/deliver/pallas_call | solution.py:609
  75.3 3.2 %multiply_convert_fusion = bf16[512,2,512]{2,0,1:T(8,128)(2,1)S(1)} fusion(bf16[2,1024,512]{2,1,0:T(8,128)(2,1)} %get-tuple-element.6, bf16[1024,512]{1,0:T(8,128)(2,1)} %get-tuple-element.5), kind=kOutput, calls=%fused_computation | convolution fusion | flops 1074790400 | bytes 4194304 | tf_op jit(solution)/shard_map/ta,btc->abc/dot_general | solution.py:647
  78.5 0.0 copy-start
  78.5 2.0 %copy.8 = bf16[512,2,512]{2,1,0:T(2,128)(2,1)} copy(bf16[512,2,512]{2,0,1:T(8,128)(2,1)S(1)} %multiply_convert_fusion) | data formatting | bytes 2097152
  80.6 0.0 copy-done
  80.6 1.0 %copy.9 = bf16[128,2,512]{2,1,0:T(2,128)(2,1)} copy(bf16[128,2,512]{2,0,1:T(8,128)(2,1)S(1)} %bitcast.7) | data formatting | bytes 524288
Async XLA Ops:
  78.5 2.1 %copy-start = (bf16[2,128,512]{2,1,0:T(8,128)(2,1)S(1)}, bf16[2,128,512]{2,1,0:T(8,128)(2,1)}, u32[]{:S(2)}) copy-start(bf16[2,128,512]{2,1,0:T(8,128)(2,1)} %get-tuple-element.7) | copy-start | bytes 786436

commit v3 on v2

--- a/solution.py
+++ b/solution.py
@@ -115,6 +115,7 @@
 
 MESH = pl.DeviceIdType.MESH
 CHUNKS = 8
+TURNED = 2
 PARTS = 4
 PLAN = (
     ("y", 0, 0), ("x", 0, 0), ("y", 0, 1), ("x", 0, 1), ("z", 1, 0), ("y", 0, 2), ("x", 0, 2),
@@ -160,9 +161,11 @@
     return (z, z + 1 - 2 * lax.rem(z, 2), 2 - z // 2, 3 - 3 * (z // 2))
 
 
-def gather_kernel(
-    pieces, out, sides, low, head, left, right, tail, rays,
-    z_send, send, recv, c_send, c_recv, local,
+def fused_kernel(
+    pieces, weight, grads, acts, product,
+    sides, low, head, left, right, tail, rays, raw, held_weight,
+    z_send, send, recv, c_send, c_recv, local, w_sem, r_send, r_recv,
+    g_send, y_send, t_send, g_recv, y_recv, a_send, a_recv, h_send, h_recv, k_send, k_recv, put,
 ):
     z, o, y, ox, oc, zs, z_peers, y_peer, x_peer, c_peer = neighbours()
     oxc = lax.rem(oc + 2, 4)
@@ -170,7 +173,7 @@
     rows = pieces.shape[1] // PARTS
     group = rows * 8
     tokens, block = sides.shape
-    part = out.shape[1]
+    part = left.shape[1]
     near = hops(z)
     across = (((1,), (1,)), ((), ()))
     sent = []
@@ -207,6 +210,22 @@
 
     d_peer = {"tok": z, "out": ox, "grp": 1 - y}
     greet(z_peers + [y_peer, x_peer, c_peer, d_peer])
+    strip = width // 2
+    strips = [(b, i) for b in range(2) for i in range(2)]
+
+    def load(n):
+        b, i = strips[n]
+        place = (b, pl.ds(i * strip, strip), slice(None))
+        return pltpu.make_async_copy(weight.at[place], held_weight.at[place], w_sem.at[n])
+
+    def raw_band(oi):
+        return raw.at[:, :, columns(oi)]
+
+    own_raw = pieces.at[2:4]
+    raw_local = pltpu.make_async_copy(own_raw, raw_band(o), r_send.at[3])
+    raw_x = remote(own_raw, raw_band(o), r_send.at[0], r_recv.at[0], x_peer)
+    raw_c = remote(own_raw, raw_band(o), r_send.at[1], r_recv.at[1], c_peer)
+    raw_xc = remote(raw_band(ox), raw_band(ox), r_send.at[2], r_recv.at[2], c_peer)
     z_sent = []
     for s in range(PARTS):
         for j in (3, 2, 1):
@@ -223,6 +242,10 @@
         owns.append(pltpu.make_async_copy(piece(z, s), tile(o, y, z, s), local.at[s]))
         owns[-1].start()
 
+    for n in range(4):
+        load(n).start()
+    raw_local.start()
+    raw_c.start()
     ones = jnp.ones((16, block), sides.dtype)
 
     def rows_of(s):
@@ -281,6 +304,7 @@
             if waiting:
                 finish(waiting.pop())
             waiting.append(s)
+    raw_x.start()
     finish(waiting.pop())
 
     def pair(a, b):
@@ -332,153 +356,108 @@
 
     left[...] = sides[:, cols]
 
-    @pl.loop(0, steps)
+    @pl.loop(0, steps, unroll=True)
     def _(i):
         value = left[span(i), :].astype(jnp.float32)
         value = 1.5 * value - 0.5 * apply(i, left, value)
         head[span(i), :] = value
         right[span(i), :] = value.astype(right.dtype)
 
-    @pl.loop(0, steps)
+    @pl.loop(0, steps, unroll=True)
     def _(i):
         value = apply(i, right, head[span(i), :])
         tail[span(i), :] = value
         left[span(i), :] = value.astype(left.dtype)
 
-    @pl.loop(0, steps)
+    @pl.loop(0, steps, unroll=True)
     def _(i):
         value = tail[span(i), :]
         value = 1.5 * value - 0.5 * apply(i, left, value)
         tail[span(i), :] = value
         right[span(i), :] = value.astype(right.dtype)
 
-    @pl.loop(0, steps)
+    raw_x.wait_recv()
+    raw_xc.start()
+
+    @pl.loop(0, steps, unroll=True)
     def _(i):
         value = tail[span(i), :]
         value = 1.5 * value - 0.5 * apply(i, right, value)
-        out[span(i), :] = ((1.5 * head[span(i), :] - 0.5 * value) * root).astype(out.dtype)
-
-    for copy in z_sent:
-        copy.wait_send()
-    for copy in sent:
-        copy.wait_send()
-    for s in range(PARTS):
-        over_core(o, s, 0).wait_send()
-        over_core(ox, s, 1).wait_send()
-
-
-def gather(pieces, part):
-    _, rows, width = pieces.shape
-    tokens, block = rows * 8, width * 4
-    dma = pltpu.SemaphoreType.DMA
-    vmem = pl.BlockSpec(memory_space=pltpu.VMEM)
-    sends = (2 * 4 + 2 * 4) * PARTS
-    return pl.pallas_call(
-        gather_kernel,
-        out_shape=jax.ShapeDtypeStruct((tokens, part), pieces.dtype),
-        in_specs=[vmem],
-        out_specs=vmem,
-        scratch_shapes=[
-            pltpu.VMEM((tokens, block), pieces.dtype),
-            pltpu.VMEM((tokens, tokens), pieces.dtype),
-            pltpu.VMEM((tokens, part), jnp.float32),
-            pltpu.VMEM((tokens, part), pieces.dtype),
-            pltpu.VMEM((tokens, part), pieces.dtype),
-            pltpu.VMEM((tokens, part), jnp.float32),
-            pltpu.VMEM((8, tokens), jnp.float32),
-            dma((3 * PARTS,)),
-            dma((sends,)),
-            dma((16 * PARTS,)),
-            dma((2 * PARTS,)),
-            dma((2 * PARTS,)),
-            dma((PARTS,)),
-        ],
-        compiler_params=pltpu.CompilerParams(collective_id=0, has_side_effects=True),
-        name="gather",
-    )(pieces)
-
-
-def deliver_kernel(
-    low, pieces, weight, grads, acts, product,
-    raw, held_weight, w_sem, r_send, r_recv, g_send, y_send, g_recv, y_recv,
-    a_send, a_recv, x_send, x_recv, c_send, c_recv, local,
-):
-    z, o, y, ox, oc, zs, z_peers, y_peer, x_peer, c_peer = neighbours()
-    tokens, part = low.shape
-    rows = tokens // CHUNKS
-    width = pieces.shape[2]
-    block = raw.shape[2]
-    strip = width // 2
-    is_grad = (z == 0) | (z == 3)
-    is_act = jnp.logical_not(is_grad)
+        left[span(i), :] = ((1.5 * head[span(i), :] - 0.5 * value) * root).astype(left.dtype)
+
+    span_rows = tokens // CHUNKS
+    is_end = is_grad == 1
+    is_middle = is_grad == 0
     mine = z // 3
     h = o // 2
     goal_z = (z // 2) * 2 + lax.rem(o, 2)
     stays = goal_z == z
     goal = {"tok": goal_z, "out": o, "grp": y}
-    near, far = z // 2, 1 - z // 2
+    first, second = z // 2, 1 - z // 2
     is_hub = lax.rem(o, 2) == lax.rem(z, 2)
-    here = is_act & stays
-    greet(z_peers + [y_peer, x_peer, c_peer])
-
-    def band(oi):
-        return raw.at[:, :, pl.ds(pl.multiple_of(oi * width, width), width)]
-
-    own_raw = pieces.at[2:4]
-    raw_local = pltpu.make_async_copy(own_raw, band(o), r_send.at[3])
-    raw_x = remote(own_raw, band(o), r_send.at[0], r_recv.at[0], x_peer)
-    raw_c = remote(own_raw, band(o), r_send.at[1], r_recv.at[1], c_peer)
-    raw_xc = remote(band(ox), band(ox), r_send.at[2], r_recv.at[2], c_peer)
-    raw_x.start()
-    raw_c.start()
-    raw_local.start()
-
-    def span(c):
-        return pl.ds(c * rows, rows)
-
-    def piece(c):
-        return low.at[span(c), :]
+    here = is_middle & stays
+    plain = [c for c in range(CHUNKS - TURNED)]
+    turned = [c for c in range(CHUNKS - TURNED, CHUNKS)]
+
+    def rung(c):
+        return pl.ds(c * span_rows, span_rows)
+
+    def piece_of(c):
+        return left.at[rung(c), :]
 
     def half(i):
         return pl.ds(pl.multiple_of(i * part, part), part)
 
     def g_tile(b, yi, c):
-        return grads.at[b, span(c), half(yi)]
+        return grads.at[b, rung(c), half(yi)]
 
     def a_tile(i, c):
-        return acts.at[span(c), half(i)]
+        return acts.at[rung(c), half(i)]
 
     def own_grad(c):
-        return pltpu.make_async_copy(piece(c), g_tile(mine, y, c), local.at[c])
+        return pltpu.make_async_copy(piece_of(c), g_tile(mine, y, c), put.at[c])
 
     def own_act(c):
-        return pltpu.make_async_copy(piece(c), a_tile(h, c), local.at[c])
+        return pltpu.make_async_copy(piece_of(c), a_tile(h, c), put.at[c])
+
+    def onward(b):
+        return {"tok": lax.rem(z + 5 - 2 * b, 4), "out": o, "grp": y}
 
     def to_plane(src, b, c):
-        return remote(src, g_tile(b, y, c), g_send.at[b * CHUNKS + c], g_recv.at[b * CHUNKS + c], {"tok": lax.rem(z + 5 - 2 * b, 4), "out": o, "grp": y})
+        n = b * CHUNKS + c
+        return remote(src, g_tile(b, y, c), g_send.at[n], g_recv.at[n], onward(b))
+
+    def other_to_plane(b, c):
+        n = b * CHUNKS + c
+        ref = g_tile(b, 1 - y, c)
+        return remote(ref, ref, t_send.at[n], y_recv.at[n], onward(b))
 
     def y_copy(src, b, c):
-        return remote(src, g_tile(b, y, c), y_send.at[b * CHUNKS + c], y_recv.at[b * CHUNKS + c], y_peer)
+        n = b * CHUNKS + c
+        return remote(src, g_tile(b, y, c), y_send.at[n], y_recv.at[n], y_peer)
 
     def to_hub(c):
-        return remote(piece(c), a_tile(h, c), a_send.at[c], a_recv.at[c], goal)
+        return remote(piece_of(c), a_tile(h, c), a_send.at[c], a_recv.at[c], goal)
 
     def over_x(c, i):
-        return remote(a_tile(i, c), a_tile(i, c), x_send.at[c], x_recv.at[c], x_peer)
-
-    def over_core(c, i):
-        place = i * CHUNKS + c
-        return remote(a_tile(i, c), a_tile(i, c), c_send.at[place], c_recv.at[place], c_peer)
+        return remote(a_tile(i, c), a_tile(i, c), h_send.at[c], h_recv.at[c], x_peer)
+
+    def act_core(c, i):
+        n = i * CHUNKS + c
+        return remote(a_tile(i, c), a_tile(i, c), k_send.at[n], k_recv.at[n], c_peer)
+
+    for b in range(2):
+
+        @pl.when(z == 3 * b)
+        def _():
+            for c in turned + plain:
+                y_copy(piece_of(c), b, c).start()
+            for c in plain + turned:
+                to_plane(piece_of(c), b, c).start()
 
     for c in range(CHUNKS):
-        for b in range(2):
-
-            @pl.when(z == 3 * b)
-            def _():
-                to_plane(piece(c), b, c).start()
-                y_copy(piece(c), b, c).start()
-
-        @pl.when(is_grad)
+
+        @pl.when(is_end)
         def _():
             own_grad(c).start()
 
@@ -486,19 +465,9 @@
         def _():
             own_act(c).start()
 
-        @pl.when(is_act & jnp.logical_not(stays))
+        @pl.when(is_middle & jnp.logical_not(stays))
         def _():
             to_hub(c).start()
-
-    strips = [(b, i) for b in range(2) for i in range(2)]
-
-    def load(n):
-        b, i = strips[n]
-        place = (b, pl.ds(i * strip, strip), slice(None))
-        return pltpu.make_async_copy(weight.at[place], held_weight.at[place], w_sem.at[n])
-
-    for n in range(4):
-        load(n).start()
 
     def multiply(n):
         b, i = strips[n]
@@ -526,60 +495,91 @@
         @pl.when(is_hub)
         def _():
             over_x(c, h).start()
-            over_core(c, h).start()
+            act_core(c, h).start()
 
     def cross_step(c):
         @pl.when(is_hub)
         def _():
             over_x(c, 1 - h).wait_recv()
-            over_core(c, 1 - h).start()
-
-    def take(b, c):
+            act_core(c, 1 - h).start()
+
+    def g_wait(b, c):
         ref = g_tile(b, y, c)
         remote(ref, ref, g_send.at[0], g_recv.at[b * CHUNKS + c], c_peer).wait_recv()
-
-        @pl.when(is_act)
-        def _():
-            to_plane(ref, b, c).start()
-
-        y_copy(ref, b, c).start()
-
-    for step in range(CHUNKS + LAG):
+        return ref
+
+    def y_wait(b, c):
+        ref = g_tile(b, 1 - y, c)
+        remote(ref, ref, y_send.at[0], y_recv.at[b * CHUNKS + c], c_peer).wait_recv()
+
+    def take(b, kind, c):
+        if kind == "own":
+            ref = g_wait(b, c)
+
+            @pl.when(is_middle)
+            def _():
+                to_plane(ref, b, c).start()
+
+            if c not in turned:
+                y_copy(ref, b, c).start()
+        else:
+            y_wait(b, c)
+
+            @pl.when(is_middle)
+            def _():
+                other_to_plane(b, c).start()
+
+    raw_local.wait()
+    raw_c.wait_recv()
+    raw_xc.wait_recv()
+    for n in range(4):
+        multiply(n)
+
+    @pl.when(is_end)
+    def _():
+        for c in turned:
+            y_wait(mine, c)
+            other_to_plane(mine, c).start()
+
+    flow = [("own", c) for c in plain + turned] + [("other", c) for c in turned]
+    for step in range(len(flow) + LAG):
+        if step < len(flow):
+
+            @pl.when(is_middle)
+            def _():
+                take(first, *flow[step])
+
         if step < CHUNKS:
-
-            @pl.when(is_act)
-            def _():
-                take(near, step)
-
             hub_step(step)
         if step >= LAG:
-            take(far, step - LAG)
-        if step == 1:
-            raw_x.wait_recv()
-            raw_xc.start()
-        if step == 2:
-            raw_c.wait_recv()
-            raw_xc.wait()
-            raw_local.wait()
-        if 3 <= step < 7:
-            multiply(step - 3)
+            take(second, *flow[step - LAG])
     for c in range(CHUNKS):
         cross_step(c)
     for c in range(CHUNKS):
         for b in range(2):
-            ref = g_tile(b, 1 - y, c)
-            remote(ref, ref, y_send.at[0], y_recv.at[b * CHUNKS + c], c_peer).wait_recv()
-            y_copy(g_tile(b, y, c), b, c).wait_send()
+            if c in turned:
+
+                @pl.when(z == 3 * b)
+                def _():
+                    y_copy(piece_of(c), b, c).wait_send()
+
+                @pl.when(z != 3 - 3 * b)
+                def _():
+                    other_to_plane(b, c).wait_send()
+
+            else:
+                y_wait(b, c)
+                y_copy(g_tile(b, y, c), b, c).wait_send()
 
             @pl.when(z != 3 - 3 * b)
             def _():
                 to_plane(g_tile(b, y, c), b, c).wait_send()
 
-        @pl.when(is_grad)
+        @pl.when(is_end)
         def _():
             own_grad(c).wait()
 
-        @pl.when(is_act & jnp.logical_not(stays))
+        @pl.when(is_middle & jnp.logical_not(stays))
         def _():
             to_hub(c).wait_send()
 
@@ -587,11 +587,11 @@
 
             @pl.when(is_hub)
             def _():
-                over_core(c, i).wait_send()
+                act_core(c, i).wait_send()
 
             @pl.when(jnp.logical_not(is_hub))
             def _():
-                over_core(c, i).wait_recv()
+                act_core(c, i).wait_recv()
 
         @pl.when(is_hub)
         def _():
@@ -599,28 +599,51 @@
 
     raw_x.wait_send()
     raw_c.wait_send()
-
-
-def deliver(low, pieces, weight):
-    tokens, part = low.shape
+    raw_xc.wait_send()
+    for copy in z_sent:
+        copy.wait_send()
+    for copy in sent:
+        copy.wait_send()
+    for s in range(PARTS):
+        over_core(o, s, 0).wait_send()
+        over_core(ox, s, 1).wait_send()
+
+
+def fused(pieces, weight, part):
     _, rows, width = pieces.shape
+    tokens, block = rows * 8, width * 4
     dma = pltpu.SemaphoreType.DMA
     vmem = pl.BlockSpec(memory_space=pltpu.VMEM)
+    low = pieces.dtype
     return pl.pallas_call(
-        deliver_kernel,
+        fused_kernel,
         out_shape=(
-            jax.ShapeDtypeStruct((2, tokens, 2 * part), low.dtype),
-            jax.ShapeDtypeStruct((tokens, 2 * part), low.dtype),
-            jax.ShapeDtypeStruct((2, rows, width), low.dtype),
+            jax.ShapeDtypeStruct((2, tokens, 2 * part), low),
+            jax.ShapeDtypeStruct((tokens, 2 * part), low),
+            jax.ShapeDtypeStruct((2, rows, width), low),
         ),
-        in_specs=[vmem, vmem, pl.BlockSpec(memory_space=pl.ANY)],
+        in_specs=[vmem, pl.BlockSpec(memory_space=pl.ANY)],
         out_specs=(vmem, vmem, vmem),
         scratch_shapes=[
-            pltpu.VMEM((2, rows, 4 * width), low.dtype),
+            pltpu.VMEM((tokens, block), low),
+            pltpu.VMEM((tokens, tokens), low),
+            pltpu.VMEM((tokens, part), jnp.float32),
+            pltpu.VMEM((tokens, part), low),
+            pltpu.VMEM((tokens, part), low),
+            pltpu.VMEM((tokens, part), jnp.float32),
+            pltpu.VMEM((8, tokens), jnp.float32),
+            pltpu.VMEM((2, rows, block), low),
             pltpu.VMEM(weight.shape, weight.dtype),
+            dma((3 * PARTS,)),
+            dma((16 * PARTS,)),
+            dma((16 * PARTS,)),
+            dma((2 * PARTS,)),
+            dma((2 * PARTS,)),
+            dma((PARTS,)),
             dma((4,)),
             dma((4,)),
             dma((3,)),
+            dma((2 * CHUNKS,)),
             dma((2 * CHUNKS,)),
             dma((2 * CHUNKS,)),
             dma((2 * CHUNKS,)),
@@ -633,9 +656,9 @@
             dma((2 * CHUNKS,)),
             dma((CHUNKS,)),
         ],
-        compiler_params=pltpu.CompilerParams(collective_id=1, has_side_effects=True),
-        name="deliver",
-    )(low, pieces, weight)
+        compiler_params=pltpu.CompilerParams(collective_id=0, has_side_effects=True),
+        name="fused",
+    )(pieces, weight)
 
 
 def planes(activations, out_grads, weight):
@@ -643,7 +666,7 @@
     part = width // lax.axis_size("grp")
     token_count = tok_dev * lax.axis_size(("tok", "grp"))
     pieces = jnp.swapaxes(jnp.concatenate([activations, out_grads], axis=1), 0, 1)
-    grads_low, acts_low, product = deliver(gather(pieces, part), pieces, weight)
+    grads_low, acts_low, product = fused(pieces, weight, part)
     update = jnp.einsum("ta,btc->abc", acts_low, grads_low, preferred_element_type=jnp.float32)
     update = (update / math.sqrt(token_count)).astype(jnp.bfloat16)
     input_grad = jnp.swapaxes(product, 0, 1)

time: 81.8 us -> 80.3 us (0.982)
  the two profiles are of different devices: /device:TPU:8 before, /device:TPU:0 now
where the time goes in v3:
time: 80.3 us; the launch traced here: 80 us
  Pallas kernels  70.4 us (88%)
  local copies, waits for them, and re-layouts  4.99 us (6%)
  matrix products  3.19 us (4%)
  other arithmetic  0.84 us (1%)
    pallas_call x1, Pallas kernels, fused(): pl.pallas_call(fused_kernel, out_shape=(jax.ShapeDtypeStruct((2, tokens,...  70.4 us
    unnamed x6, local copies, waits for them, and re-layouts  4.99 us
    dot_general x1, matrix products, planes(): jnp.einsum('ta,btc->abc', acts_low, grads_low, preferred_element_type=jnp...  3.19 us

profile of v3, /device:TPU:0, one launch (start us, length us, event | category | flops | bytes accessed | tf_op | source)
XLA Modules:
  0.0 80.0 jit_solution(16303104191424354088)
XLA Ops:
  0.6 1.0 %copy.5 = bf16[128,2,512]{2,0,1:T(8,128)(2,1)S(1)} copy(bf16[128,2,512]{2,1,0:T(2,128)(2,1)} %param.3) | data formatting | bytes 524288 | tf_op args[0]
  1.6 1.0 %copy.6 = bf16[128,2,512]{2,0,1:T(8,128)(2,1)S(1)} copy(bf16[128,2,512]{2,1,0:T(2,128)(2,1)} %param.4) | data formatting | bytes 524288 | tf_op args[1]
  2.6 0.8 %maximum_bitcast_fusion.pieces = bf16[4,128,512]{2,1,0:T(8,128)(2,1)} fusion(bf16[128,2,512]{2,0,1:T(8,128)(2,1)S(1)} %copy.6, bf16[128,2,512]{2,0,1:T(8,128)(2,1)S(1)} %copy.5), kind=kLoop, calls=%fused_computation.2 | loop fusion | flops 262144 | bytes 1048576 | tf_op jit(solution)/shard_map/transpose | solution.py:668
  3.4 70.4 %fused.1 = (bf16[2,1024,512]{2,1,0:T(8,128)(2,1)}, bf16[1024,512]{1,0:T(8,128)(2,1)}, bf16[2,128,512]{2,1,0:T(8,128)(2,1)}) custom-call(bf16[4,128,512]{2,1,0:T(8,128)(2,1)} %maximum_bitcast_fusion.pieces, bf16[2,512,4096]{2,1,0:T(8,128)(2,1)} %weight.1), custom_call_target="tpu_custom_call" | custom-call | tf_op jit(solution)/shard_map/fused/pallas_call | solution.py:618
  73.8 3.2 %multiply_convert_fusion = bf16[512,2,512]{2,0,1:T(8,128)(2,1)S(1)} fusion(bf16[2,1024,512]{2,1,0:T(8,128)(2,1)} %get-tuple-element.6, bf16[1024,512]{1,0:T(8,128)(2,1)} %get-tuple-element.5), kind=kOutput, calls=%fused_computation | convolution fusion | flops 1074790400 | bytes 4194304 | tf_op jit(solution)/shard_map/ta,btc->abc/dot_general | solution.py:670
  77.0 0.0 copy-start
  77.0 2.0 %copy.8 = bf16[512,2,512]{2,1,0:T(2,128)(2,1)} copy(bf16[512,2,512]{2,0,1:T(8,128)(2,1)S(1)} %multiply_convert_fusion) | data formatting | bytes 2097152
  79.1 0.0 copy-done
  79.1 1.0 %copy.9 = bf16[128,2,512]{2,1,0:T(2,128)(2,1)} copy(bf16[128,2,512]{2,0,1:T(8,128)(2,1)S(1)} %bitcast.7) | data formatting | bytes 524288
Async XLA Ops:
  77.0 2.1 %copy-start = (bf16[2,128,512]{2,1,0:T(8,128)(2,1)S(1)}, bf16[2,128,512]{2,1,0:T(8,128)(2,1)}, u32[]{:S(2)}) copy-start(bf16[2,128,512]{2,1,0:T(8,128)(2,1)} %get-tuple-element.7) | copy-start | bytes 786436

commit v4 on v3

--- a/solution.py
+++ b/solution.py
@@ -116,6 +116,7 @@
 MESH = pl.DeviceIdType.MESH
 CHUNKS = 8
 TURNED = 2
+ROOM = 50 * 2**20
 PARTS = 4
 PLAN = (
     ("y", 0, 0), ("x", 0, 0), ("y", 0, 1), ("x", 0, 1), ("z", 1, 0), ("y", 0, 2), ("x", 0, 2),
@@ -376,9 +377,6 @@
         tail[span(i), :] = value
         right[span(i), :] = value.astype(right.dtype)
 
-    raw_x.wait_recv()
-    raw_xc.start()
-
     @pl.loop(0, steps, unroll=True)
     def _(i):
         value = tail[span(i), :]
@@ -529,11 +527,15 @@
             def _():
                 other_to_plane(b, c).start()
 
+    raw_x.wait_recv()
+    raw_xc.start()
     raw_local.wait()
     raw_c.wait_recv()
-    raw_xc.wait_recv()
-    for n in range(4):
-        multiply(n)
+
+    def multiply_all():
+        raw_xc.wait_recv()
+        for n in range(4):
+            multiply(n)
 
     @pl.when(is_end)
     def _():
@@ -541,6 +543,7 @@
             y_wait(mine, c)
             other_to_plane(mine, c).start()
 
+    pl.when(is_end)(multiply_all)
     flow = [("own", c) for c in plain + turned] + [("other", c) for c in turned]
     for step in range(len(flow) + LAG):
         if step < len(flow):
@@ -555,6 +558,7 @@
             take(second, *flow[step - LAG])
     for c in range(CHUNKS):
         cross_step(c)
+    pl.when(is_middle)(multiply_all)
     for c in range(CHUNKS):
         for b in range(2):
             if c in turned:
@@ -622,7 +626,7 @@
             jax.ShapeDtypeStruct((tokens, 2 * part), low),
             jax.ShapeDtypeStruct((2, rows, width), low),
         ),
-        in_specs=[vmem, pl.BlockSpec(memory_space=pl.ANY)],
+        in_specs=[vmem, pl.BlockSpec(memory_space=pltpu.HBM)],
         out_specs=(vmem, vmem, vmem),
         scratch_shapes=[
             pltpu.VMEM((tokens, block), low),
@@ -656,7 +660,7 @@
             dma((2 * CHUNKS,)),
             dma((CHUNKS,)),
         ],
-        compiler_params=pltpu.CompilerParams(collective_id=0, has_side_effects=True),
+        compiler_params=pltpu.CompilerParams(collective_id=0, has_side_effects=True, vmem_limit_bytes=ROOM),
         name="fused",
     )(pieces, weight)
 

time: 80.3 us -> 69.3 us (0.86)
  Pallas kernels: 70.4 us -> 62.2 us
  matrix products: 3.19 us -> 1.27 us
    pallas_call x1, Pallas kernels: 70.4 us -> 62.2 us  [fused(): pl.pallas_call(fused_kernel, out_shape=(jax.ShapeDtypeStruct((2, tokens,...]
    dot_general x1, matrix products: 3.19 us -> 1.27 us  [planes(): jnp.einsum('ta,btc->abc', acts_low, grads_low, preferred_element_type=jnp...]
    unnamed x6 -> x4, local copies, waits for them, and re-layouts: 4.99 us -> 4.98 us
where the time goes in v4:
time: 69.3 us; the launch traced here: 69.1 us
  Pallas kernels  62.2 us (90%)
  local copies, waits for them, and re-layouts  4.98 us (7%)
  matrix products  1.27 us (2%)
    pallas_call x1, Pallas kernels, fused(): pl.pallas_call(fused_kernel, out_shape=(jax.ShapeDtypeStruct((2, tokens,...  62.2 us
    unnamed x4, local copies, waits for them, and re-layouts  4.98 us

profile of v4, /device:TPU:0, one launch (start us, length us, event | category | flops | bytes accessed | tf_op | source)
XLA Modules:
  0.0 69.1 jit_solution(1682653953931023511)
XLA Ops:
  0.6 1.0 %copy.5 = bf16[128,2,512]{2,0,1:T(8,128)(2,1)S(1)} copy(bf16[128,2,512]{2,1,0:T(2,128)(2,1)} %param.3) | data formatting | bytes 524288 | tf_op args[0]
  1.6 1.0 %copy.6 = bf16[128,2,512]{2,0,1:T(8,128)(2,1)S(1)} copy(bf16[128,2,512]{2,1,0:T(2,128)(2,1)} %param.4) | data formatting | bytes 524288 | tf_op args[1]
  2.7 62.2 %fused.1 = (bf16[2,1024,512]{2,1,0:T(8,128)(2,1)S(1)}, bf16[1024,512]{1,0:T(8,128)(2,1)S(1)}, bf16[2,128,512]{2,1,0:T(8,128)(2,1)S(1)}) custom-call(bf16[4,128,512]{2,1,0:T(8,128)(2,1)S(1)} %maximum_bitcast_fusion.pieces, bf16[2,512,4096]{2,1,0:T(8,128)(2,1)} %weight.1), custom_call_target="tpu_custom_call" | custom-call | tf_op jit(solution)/shard_map/fused/pallas_call | solution.py:622
  64.8 1.3 %multiply_convert_fusion = bf16[512,2,512]{2,0,1:T(8,128)(2,1)S(1)} fusion(bf16[2,1024,512]{2,1,0:T(8,128)(2,1)S(1)} %get-tuple-element.6, bf16[1024,512]{1,0:T(8,128)(2,1)S(1)} %get-tuple-element.5), kind=kOutput, calls=%fused_computation | convolution fusion | flops 1074790400 | bytes 4194304 | tf_op jit(solution)/shard_map/ta,btc->abc/dot_general | solution.py:674
  66.1 2.0 %copy.8 = bf16[512,2,512]{2,1,0:T(2,128)(2,1)} copy(bf16[512,2,512]{2,0,1:T(8,128)(2,1)S(1)} %multiply_convert_fusion) | data formatting | bytes 2097152
  68.1 1.0 %copy.9 = bf16[128,2,512]{2,1,0:T(2,128)(2,1)} copy(bf16[128,2,512]{2,0,1:T(8,128)(2,1)S(1)} %bitcast.7) | data formatting | bytes 524288
  (1 shorter events, 0.0 us)

commit v5 on v4

--- a/solution.py
+++ b/solution.py
@@ -116,6 +116,7 @@
 MESH = pl.DeviceIdType.MESH
 CHUNKS = 8
 TURNED = 2
+CORNER = 3
 ROOM = 50 * 2**20
 PARTS = 4
 PLAN = (
@@ -165,8 +166,8 @@
 def fused_kernel(
     pieces, weight, grads, acts, product,
     sides, low, head, left, right, tail, rays, raw, held_weight,
-    z_send, send, recv, c_send, c_recv, local, w_sem, r_send, r_recv,
-    g_send, y_send, t_send, g_recv, y_recv, a_send, a_recv, h_send, h_recv, k_send, k_recv, put,
+    z_send, send, recv, d_recv, c_send, c_recv, local, w_sem, r_send, r_recv,
+    g_send, y_send, t_send, g_recv, y_recv, t_recv, a_send, a_recv, h_send, h_recv, k_send, k_recv, put,
 ):
     z, o, y, ox, oc, zs, z_peers, y_peer, x_peer, c_peer = neighbours()
     oxc = lax.rem(oc + 2, 4)
@@ -189,17 +190,23 @@
     def piece(zi, s):
         return pieces.at[held(zi), pl.ds(s * rows, rows), :]
 
-    def sem_of(oi, yi, zi, s):
-        return recv.at[((oi // 2) * 8 + yi * 4 + zi) * PARTS + s]
-
-    def push(src, where, peer):
-        copy = remote(src, tile(*where), send.at[len(sent)], sem_of(*where), peer)
-        copy.start()
-        sent.append(copy)
-
-    def arrived(*where):
+    def sem_of(kind, zi, s):
+        if kind == CORNER:
+            return d_recv.at[s]
+        return recv.at[(kind * 4 + zi) * PARTS + s]
+
+    def push(src, where, kind):
+        peer = (None, y_peer, x_peer, d_peer)[kind]
+        remote(src, tile(*where), send.at[0], sem_of(kind, where[2], where[3]), peer).start()
+        sent.append(where)
+
+    def relay(src, where, kind, peer):
+        remote(src, tile(*where), send.at[0], sem_of(kind, where[2], where[3]), peer).start()
+        sent.append(where)
+
+    def arrived(kind, *where):
         ref = tile(*where)
-        remote(ref, ref, send.at[0], sem_of(*where), c_peer).wait_recv()
+        remote(ref, ref, send.at[0], sem_of(kind, where[2], where[3]), c_peer).wait_recv()
         return ref
 
     def band(oi, s):
@@ -207,7 +214,7 @@
 
     def over_core(oi, s, place):
         n = s * 2 + place
-        return remote(band(oi, s), band(oi, s), c_send.at[n], c_recv.at[n], c_peer)
+        return remote(band(oi, s), band(oi, s), c_send.at[0], c_recv.at[n], c_peer)
 
     d_peer = {"tok": z, "out": ox, "grp": 1 - y}
     greet(z_peers + [y_peer, x_peer, c_peer, d_peer])
@@ -227,21 +234,17 @@
     raw_x = remote(own_raw, raw_band(o), r_send.at[0], r_recv.at[0], x_peer)
     raw_c = remote(own_raw, raw_band(o), r_send.at[1], r_recv.at[1], c_peer)
     raw_xc = remote(raw_band(ox), raw_band(ox), r_send.at[2], r_recv.at[2], c_peer)
-    z_sent = []
     for s in range(PARTS):
         for j in (3, 2, 1):
             copy = remote(
-                piece(near[j], s), tile(o, y, z, s), z_send.at[len(z_sent)], sem_of(o, y, z, s),
+                piece(near[j], s), tile(o, y, z, s), z_send.at[0], sem_of(0, z, s),
                 {"tok": near[j], "out": o, "grp": y},
             )
             copy.start()
-            z_sent.append(copy)
-        push(piece(z, s), (o, y, z, s), y_peer)
-        push(piece(z, s), (o, y, z, s), x_peer)
-    owns = []
+        push(piece(z, s), (o, y, z, s), 1)
+        push(piece(z, s), (o, y, z, s), 2)
     for s in range(PARTS):
-        owns.append(pltpu.make_async_copy(piece(z, s), tile(o, y, z, s), local.at[s]))
-        owns[-1].start()
+        pltpu.make_async_copy(piece(z, s), tile(o, y, z, s), local.at[0]).start()
 
     for n in range(4):
         load(n).start()
@@ -276,31 +279,35 @@
         known.append(s)
 
     known = []
+    placed = []
     waiting = []
     for kind, j, s in PLAN:
         if kind == "z":
             where = (o, y, near[j], s)
-            ref = arrived(*where)
-            push(ref, where, y_peer)
-            push(ref, where, x_peer)
+            ref = arrived(0, *where)
+            push(ref, where, 1)
+            push(ref, where, 2)
             if straight(j, s):
-                push(ref, where, d_peer)
+                push(ref, where, CORNER)
         elif kind == "y":
             where = (o, 1 - y, near[j], s)
-            ref = arrived(*where)
+            ref = arrived(1, *where)
             if (j + s) % 2 == 0 and not straight(j, s):
-                push(ref, where, x_peer)
+                relay(ref, where, CORNER, x_peer)
         elif kind == "x":
             where = (ox, y, near[j], s)
-            ref = arrived(*where)
+            ref = arrived(2, *where)
             if (j + s) % 2 == 1 and not straight(j, s):
-                push(ref, where, y_peer)
+                relay(ref, where, CORNER, y_peer)
         elif kind == "c":
-            owns[s].wait()
+            if not placed:
+                pltpu.make_async_copy(pieces.at[0], pieces.at[0], local.at[0]).wait()
+                placed.append(s)
             over_core(o, s, 0).start()
         else:
-            for i in range(4):
-                arrived(ox, 1 - y, near[i], s)
+            corner = pl.multiple_of((s * 2 + 1 - y) * 4 * rows, rows)
+            ref = sides.at[pl.ds(corner, 4 * rows), columns(ox)]
+            remote(ref, ref, send.at[0], d_recv.at[s], c_peer).wait_recv()
             over_core(ox, s, 1).start()
             if waiting:
                 finish(waiting.pop())
@@ -412,37 +419,39 @@
     def a_tile(i, c):
         return acts.at[rung(c), half(i)]
 
-    def own_grad(c):
-        return pltpu.make_async_copy(piece_of(c), g_tile(mine, y, c), put.at[c])
-
-    def own_act(c):
-        return pltpu.make_async_copy(piece_of(c), a_tile(h, c), put.at[c])
+    def own_grad():
+        return pltpu.make_async_copy(left, grads.at[mine, :, half(y)], put.at[0])
+
+    def own_act():
+        return pltpu.make_async_copy(left, acts.at[:, half(h)], put.at[0])
 
     def onward(b):
         return {"tok": lax.rem(z + 5 - 2 * b, 4), "out": o, "grp": y}
 
     def to_plane(src, b, c):
         n = b * CHUNKS + c
-        return remote(src, g_tile(b, y, c), g_send.at[n], g_recv.at[n], onward(b))
+        return remote(src, g_tile(b, y, c), g_send.at[b], g_recv.at[n], onward(b))
+
+    def lands(b, c):
+        if c in turned:
+            return t_recv.at[b * TURNED + turned.index(c)]
+        return y_recv.at[b]
 
     def other_to_plane(b, c):
-        n = b * CHUNKS + c
         ref = g_tile(b, 1 - y, c)
-        return remote(ref, ref, t_send.at[n], y_recv.at[n], onward(b))
+        return remote(ref, ref, t_send.at[b], lands(b, c), onward(b))
 
     def y_copy(src, b, c):
-        n = b * CHUNKS + c
-        return remote(src, g_tile(b, y, c), y_send.at[n], y_recv.at[n], y_peer)
+        return remote(src, g_tile(b, y, c), y_send.at[b], lands(b, c), y_peer)
 
     def to_hub(c):
-        return remote(piece_of(c), a_tile(h, c), a_send.at[c], a_recv.at[c], goal)
+        return remote(piece_of(c), a_tile(h, c), a_send.at[0], a_recv.at[c], goal)
 
     def over_x(c, i):
-        return remote(a_tile(i, c), a_tile(i, c), h_send.at[c], h_recv.at[c], x_peer)
+        return remote(a_tile(i, c), a_tile(i, c), h_send.at[0], h_recv.at[c], x_peer)
 
     def act_core(c, i):
-        n = i * CHUNKS + c
-        return remote(a_tile(i, c), a_tile(i, c), k_send.at[n], k_recv.at[n], c_peer)
+        return remote(a_tile(i, c), a_tile(i, c), k_send.at[0], k_recv.at[0], c_peer)
 
     for b in range(2):
 
@@ -453,18 +462,17 @@
             for c in plain + turned:
                 to_plane(piece_of(c), b, c).start()
 
-    for c in range(CHUNKS):
-
-        @pl.when(is_end)
-        def _():
-            own_grad(c).start()
-
-        @pl.when(here)
-        def _():
-            own_act(c).start()
-
-        @pl.when(is_middle & jnp.logical_not(stays))
-        def _():
+    @pl.when(is_end)
+    def _():
+        own_grad().start()
+
+    @pl.when(here)
+    def _():
+        own_act().start()
+
+    @pl.when(is_middle & jnp.logical_not(stays))
+    def _():
+        for c in range(CHUNKS):
             to_hub(c).start()
 
     def multiply(n):
@@ -481,9 +489,11 @@
         product[b, :, pl.ds(i * strip, strip)] = total.astype(product.dtype)
 
     def hub_step(c):
-        @pl.when(here)
-        def _():
-            own_act(c).wait()
+        if c == 0:
+
+            @pl.when(here)
+            def _():
+                own_act().wait()
 
         @pl.when(is_hub & jnp.logical_not(here))
         def _():
@@ -508,7 +518,7 @@
 
     def y_wait(b, c):
         ref = g_tile(b, 1 - y, c)
-        remote(ref, ref, y_send.at[0], y_recv.at[b * CHUNKS + c], c_peer).wait_recv()
+        remote(ref, ref, y_send.at[0], lands(b, c), c_peer).wait_recv()
 
     def take(b, kind, c):
         if kind == "own":
@@ -559,58 +569,52 @@
     for c in range(CHUNKS):
         cross_step(c)
     pl.when(is_middle)(multiply_all)
-    for c in range(CHUNKS):
-        for b in range(2):
-            if c in turned:
-
-                @pl.when(z == 3 * b)
-                def _():
-                    y_copy(piece_of(c), b, c).wait_send()
-
-                @pl.when(z != 3 - 3 * b)
-                def _():
-                    other_to_plane(b, c).wait_send()
-
-            else:
-                y_wait(b, c)
-                y_copy(g_tile(b, y, c), b, c).wait_send()
-
-            @pl.when(z != 3 - 3 * b)
-            def _():
-                to_plane(g_tile(b, y, c), b, c).wait_send()
-
-        @pl.when(is_end)
+    straight_rows = pl.ds(0, span_rows * len(plain))
+    turned_rows = pl.ds(span_rows * len(plain), span_rows * TURNED)
+
+    def settle(ref, sem):
+        remote(ref, ref, sem, sem, c_peer).wait_send()
+
+    for b in range(2):
+        ref = grads.at[b, straight_rows, half(1 - y)]
+        remote(ref, ref, y_send.at[0], y_recv.at[b], c_peer).wait_recv()
+
+        @pl.when(z == 3 * b)
         def _():
-            own_grad(c).wait()
-
-        @pl.when(is_middle & jnp.logical_not(stays))
+            settle(left, y_send.at[b])
+
+        @pl.when(z != 3 * b)
         def _():
-            to_hub(c).wait_send()
-
-        for i in range(2):
-
-            @pl.when(is_hub)
-            def _():
-                act_core(c, i).wait_send()
-
-            @pl.when(jnp.logical_not(is_hub))
-            def _():
-                act_core(c, i).wait_recv()
-
-        @pl.when(is_hub)
+            settle(grads.at[b, straight_rows, half(y)], y_send.at[b])
+
+        @pl.when(z != 3 - 3 * b)
         def _():
-            over_x(c, h).wait_send()
+            settle(left, g_send.at[b])
+            settle(grads.at[b, turned_rows, half(1 - y)], t_send.at[b])
+
+    @pl.when(is_end)
+    def _():
+        own_grad().wait()
+
+    @pl.when(is_middle & jnp.logical_not(stays))
+    def _():
+        settle(left, a_send.at[0])
+
+    @pl.when(is_hub)
+    def _():
+        settle(acts, k_send.at[0])
+        settle(acts.at[:, half(h)], h_send.at[0])
+
+    @pl.when(jnp.logical_not(is_hub))
+    def _():
+        remote(acts, acts, k_send.at[0], k_recv.at[0], c_peer).wait_recv()
 
     raw_x.wait_send()
     raw_c.wait_send()
     raw_xc.wait_send()
-    for copy in z_sent:
-        copy.wait_send()
-    for copy in sent:
-        copy.wait_send()
-    for s in range(PARTS):
-        over_core(o, s, 0).wait_send()
-        over_core(ox, s, 1).wait_send()
+    settle(pieces.at[0:3], z_send.at[0])
+    settle(sides.at[pl.ds(0, len(sent) * rows * width // block), :], send.at[0])
+    settle(sides.at[pl.ds(0, tokens // 2), :], c_send.at[0])
 
 
 def fused(pieces, weight, part):
@@ -638,27 +642,29 @@
             pltpu.VMEM((8, tokens), jnp.float32),
             pltpu.VMEM((2, rows, block), low),
             pltpu.VMEM(weight.shape, weight.dtype),
-            dma((3 * PARTS,)),
-            dma((16 * PARTS,)),
-            dma((16 * PARTS,)),
+            dma((1,)),
+            dma((1,)),
+            dma((12 * PARTS,)),
+            dma((PARTS,)),
+            dma((1,)),
             dma((2 * PARTS,)),
-            dma((2 * PARTS,)),
-            dma((PARTS,)),
+            dma((1,)),
             dma((4,)),
             dma((4,)),
             dma((3,)),
+            dma((2,)),
+            dma((2,)),
+            dma((2,)),
             dma((2 * CHUNKS,)),
-            dma((2 * CHUNKS,)),
-            dma((2 * CHUNKS,)),
-            dma((2 * CHUNKS,)),
-            dma((2 * CHUNKS,)),
+            dma((2,)),
+            dma((2 * TURNED,)),
+            dma((1,)),
             dma((CHUNKS,)),
+            dma((1,)),
             dma((CHUNKS,)),
-            dma((CHUNKS,)),
-            dma((CHUNKS,)),
-            dma((2 * CHUNKS,)),
-            dma((2 * CHUNKS,)),
-            dma((CHUNKS,)),
+            dma((1,)),
+            dma((1,)),
+            dma((1,)),
         ],
         compiler_params=pltpu.CompilerParams(collective_id=0, has_side_effects=True, vmem_limit_bytes=ROOM),
         name="fused",

time: 69.3 us -> 67.4 us (0.973)
  Pallas kernels: 62.2 us -> 60.3 us
    pallas_call x1, Pallas kernels: 62.2 us -> 60.3 us  [fused(): pl.pallas_call(fused_kernel, out_shape=(jax.ShapeDtypeStruct((2, tokens,...]
where the time goes in v5:
time: 67.4 us; the launch traced here: 67.2 us
  Pallas kernels  60.3 us (89%)
  local copies, waits for them, and re-layouts  4.98 us (7%)
  matrix products  1.27 us (2%)
    pallas_call x1, Pallas kernels, fused(): pl.pallas_call(fused_kernel, out_shape=(jax.ShapeDtypeStruct((2, tokens,...  60.3 us
    unnamed x4, local copies, waits for them, and re-layouts  4.98 us

profile of v5, /device:TPU:0, one launch (start us, length us, event | category | flops | bytes accessed | tf_op | source)
XLA Modules:
  0.0 67.2 jit_solution(9530950434735744638)
XLA Ops:
  0.6 1.0 %copy.5 = bf16[128,2,512]{2,0,1:T(8,128)(2,1)S(1)} copy(bf16[128,2,512]{2,1,0:T(2,128)(2,1)} %param.3) | data formatting | bytes 524288 | tf_op args[0]
  1.6 1.0 %copy.6 = bf16[128,2,512]{2,0,1:T(8,128)(2,1)S(1)} copy(bf16[128,2,512]{2,1,0:T(2,128)(2,1)} %param.4) | data formatting | bytes 524288 | tf_op args[1]
  2.7 60.3 %fused.1 = (bf16[2,1024,512]{2,1,0:T(8,128)(2,1)S(1)}, bf16[1024,512]{1,0:T(8,128)(2,1)S(1)}, bf16[2,128,512]{2,1,0:T(8,128)(2,1)S(1)}) custom-call(bf16[4,128,512]{2,1,0:T(8,128)(2,1)S(1)} %maximum_bitcast_fusion.pieces, bf16[2,512,4096]{2,1,0:T(8,128)(2,1)} %weight.1), custom_call_target="tpu_custom_call" | custom-call | tf_op jit(solution)/shard_map/fused/pallas_call | solution.py:626
  62.9 1.3 %multiply_convert_fusion = bf16[512,2,512]{2,0,1:T(8,128)(2,1)S(1)} fusion(bf16[2,1024,512]{2,1,0:T(8,128)(2,1)S(1)} %get-tuple-element.6, bf16[1024,512]{1,0:T(8,128)(2,1)S(1)} %get-tuple-element.5), kind=kOutput, calls=%fused_computation | convolution fusion | flops 1074790400 | bytes 4194304 | tf_op jit(solution)/shard_map/ta,btc->abc/dot_general | solution.py:680
  64.2 2.0 %copy.8 = bf16[512,2,512]{2,1,0:T(2,128)(2,1)} copy(bf16[512,2,512]{2,0,1:T(8,128)(2,1)S(1)} %multiply_convert_fusion) | data formatting | bytes 2097152
  66.3 1.0 %copy.9 = bf16[128,2,512]{2,1,0:T(2,128)(2,1)} copy(bf16[128,2,512]{2,0,1:T(8,128)(2,1)S(1)} %bitcast.7) | data formatting | bytes 524288
  (1 shorter events, 0.0 us)

commit v6 on v5

--- a/solution.py
+++ b/solution.py
@@ -115,9 +115,10 @@
 
 MESH = pl.DeviceIdType.MESH
 CHUNKS = 8
-TURNED = 2
+TURNED = 1
 CORNER = 3
 ROOM = 50 * 2**20
+STEPS = 2
 PARTS = 4
 PLAN = (
     ("y", 0, 0), ("x", 0, 0), ("y", 0, 1), ("x", 0, 1), ("z", 1, 0), ("y", 0, 2), ("x", 0, 2),
@@ -129,7 +130,7 @@
     ("y", 3, 2), ("c", 0, 2), ("x", 2, 3), ("d", 0, 1), ("y", 2, 3), ("x", 3, 3), ("y", 3, 3),
     ("c", 0, 3), ("d", 0, 2), ("d", 0, 3),
 )
-LAG = 3
+LAG = 2
 
 
 def greet(peers):
@@ -475,7 +476,7 @@
         for c in range(CHUNKS):
             to_hub(c).start()
 
-    def multiply(n):
+    def strip_product(n):
         b, i = strips[n]
         load(n).wait()
         total = jnp.zeros((raw.shape[1], strip), jnp.float32)
@@ -486,7 +487,11 @@
                 (((1,), (1,)), ((), ())),
                 preferred_element_type=jnp.float32,
             )
-        product[b, :, pl.ds(i * strip, strip)] = total.astype(product.dtype)
+        return total
+
+    def multiply(i):
+        pair_of = jnp.stack([strip_product(i), strip_product(2 + i)], axis=1)
+        product[:, :, pl.ds(i * strip, strip)] = pair_of.astype(product.dtype)
 
     def hub_step(c):
         if c == 0:
@@ -544,8 +549,8 @@
 
     def multiply_all():
         raw_xc.wait_recv()
-        for n in range(4):
-            multiply(n)
+        for i in range(2):
+            multiply(i)
 
     @pl.when(is_end)
     def _():
@@ -628,7 +633,7 @@
         out_shape=(
             jax.ShapeDtypeStruct((2, tokens, 2 * part), low),
             jax.ShapeDtypeStruct((tokens, 2 * part), low),
-            jax.ShapeDtypeStruct((2, rows, width), low),
+            jax.ShapeDtypeStruct((rows, 2, width), low),
         ),
         in_specs=[vmem, pl.BlockSpec(memory_space=pltpu.HBM)],
         out_specs=(vmem, vmem, vmem),
@@ -671,16 +676,60 @@
     )(pieces, weight)
 
 
+def update_kernel(grads, acts, product, update, input_grad, sem):
+    i = pl.program_id(0)
+    tokens = acts.shape[0]
+    tall = update.shape[0]
+    copy = pltpu.make_async_copy(product, input_grad, sem)
+
+    @pl.when(i == 0)
+    def _():
+        copy.start()
+
+    left = acts[:, pl.ds(pl.multiple_of(i * tall, tall), tall)]
+    down = (((0,), (0,)), ((), ()))
+    both = [
+        lax.dot_general(left, grads[b], down, preferred_element_type=jnp.float32)
+        * (1.0 / math.sqrt(tokens))
+        for b in range(2)
+    ]
+    update[...] = jnp.stack([u.astype(update.dtype) for u in both], axis=1)
+
+    @pl.when(i == pl.num_programs(0) - 1)
+    def _():
+        copy.wait()
+
+
+def update_product(grads, acts, product):
+    count, tokens, width = grads.shape
+    height = acts.shape[1]
+    tall = height // STEPS
+    vmem = pl.BlockSpec(memory_space=pltpu.VMEM)
+    return pl.pallas_call(
+        update_kernel,
+        grid=(STEPS,),
+        out_shape=(
+            jax.ShapeDtypeStruct((height, count, width), grads.dtype),
+            jax.ShapeDtypeStruct(product.shape, product.dtype),
+        ),
+        in_specs=[vmem, vmem, vmem],
+        out_specs=(
+            pl.BlockSpec((tall, count, width), lambda i: (i, 0, 0)),
+            pl.BlockSpec(memory_space=pl.ANY),
+        ),
+        scratch_shapes=[pltpu.SemaphoreType.DMA],
+        compiler_params=pltpu.CompilerParams(vmem_limit_bytes=ROOM),
+        name="update",
+    )(grads, acts, product)
+
+
 def planes(activations, out_grads, weight):
     tok_dev, _, width = activations.shape
     part = width // lax.axis_size("grp")
     token_count = tok_dev * lax.axis_size(("tok", "grp"))
     pieces = jnp.swapaxes(jnp.concatenate([activations, out_grads], axis=1), 0, 1)
     grads_low, acts_low, product = fused(pieces, weight, part)
-    update = jnp.einsum("ta,btc->abc", acts_low, grads_low, preferred_element_type=jnp.float32)
-    update = (update / math.sqrt(token_count)).astype(jnp.bfloat16)
-    input_grad = jnp.swapaxes(product, 0, 1)
-    return (update, input_grad)
+    return update_product(grads_low, acts_low, product)
 
 
 def solution(mesh):

time: 67.4 us -> 64.9 us (0.963)
  local copies, waits for them, and re-layouts: 4.98 us -> 1.96 us
  Pallas kernels: 60.3 us -> 61.9 us
  matrix products: 1.27 us -> 0 us
    pallas_call x0 -> x1, Pallas kernels: none -> 3.79 us  [update_product(): pl.pallas_call(update_kernel, grid=(STEPS,), out_shape=(jax.ShapeDtypeStr...]
    unnamed x4 -> x2, local copies, waits for them, and re-layouts: 4.98 us -> 1.96 us
    pallas_call x1, Pallas kernels: 60.3 us -> 58.1 us  [fused(): pl.pallas_call(fused_kernel, out_shape=(jax.ShapeDtypeStruct((2, tokens,...]
    dot_general x1 -> x0, matrix products: 1.27 us -> none  [planes(): jnp.einsum('ta,btc->abc', acts_low, grads_low, preferred_element_type=jnp...]
where the time goes in v6:
time: 64.9 us; the launch traced here: 64.7 us
  Pallas kernels  61.9 us (95%)
  local copies, waits for them, and re-layouts  1.96 us (3%)
  between operations  0.81 us (1%)
    pallas_call x1, Pallas kernels, fused(): pl.pallas_call(fused_kernel, out_shape=(jax.ShapeDtypeStruct((2, tokens,...  58.1 us
    pallas_call x1, Pallas kernels, update_product(): pl.pallas_call(update_kernel, grid=(STEPS,), out_shape=(jax.ShapeDtypeStr...  3.79 us
    unnamed x2, local copies, waits for them, and re-layouts  1.96 us

profile of v6, /device:TPU:0, one launch (start us, length us, event | category | flops | bytes accessed | tf_op | source)
XLA Modules:
  0.0 64.7 jit_solution(6812450499683492539)
XLA Ops:
  0.6 1.0 %copy.5 = bf16[128,2,512]{2,0,1:T(8,128)(2,1)S(1)} copy(bf16[128,2,512]{2,1,0:T(2,128)(2,1)} %param.3) | data formatting | bytes 524288 | tf_op args[0]
  1.6 1.0 %copy.6 = bf16[128,2,512]{2,0,1:T(8,128)(2,1)S(1)} copy(bf16[128,2,512]{2,1,0:T(2,128)(2,1)} %param.4) | data formatting | bytes 524288 | tf_op args[1]
  2.7 58.1 %fused.1 = (bf16[2,1024,512]{2,1,0:T(8,128)(2,1)S(1)}, bf16[1024,512]{1,0:T(8,128)(2,1)S(1)}, bf16[128,2,512]{2,1,0:T(2,128)(2,1)S(1)}) custom-call(bf16[4,128,512]{2,1,0:T(8,128)(2,1)S(1)} %maximum_bitcast_fusion.pieces, bf16[2,512,4096]{2,1,0:T(8,128)(2,1)} %weight.1), custom_call_target="tpu_custom_call" | custom-call | tf_op jit(solution)/shard_map/fused/pallas_call | solution.py:631
  60.8 3.8 %update.1 = (bf16[512,2,512]{2,1,0:T(2,128)(2,1)}, bf16[128,2,512]{2,1,0:T(2,128)(2,1)}) custom-call(bf16[2,1024,512]{2,1,0:T(8,128)(2,1)S(1)} %get-tuple-element.5.grads, bf16[1024,512]{1,0:T(8,128)(2,1)S(1)} %get-tuple-element.6.acts, bf16[128,2,512]{2,1,0:T(2,128)(2,1)S(1)} %get-tuple-element.7.product), custom_call_target="tpu_custom_call" | custom-call | tf_op jit(solution)/shard_map/update/pallas_call | solution.py:708
  (1 shorter events, 0.0 us)

commit v7 on v6

--- a/solution.py
+++ b/solution.py
@@ -133,10 +133,11 @@
 LAG = 2
 
 
-def greet(peers):
+def greet(peers, meanwhile):
     barrier = pltpu.get_barrier_semaphore()
     for peer in peers:
         pl.semaphore_signal(barrier, inc=1, device_id=peer, device_id_type=MESH)
+    meanwhile()
     pl.semaphore_wait(barrier, len(peers))
 
 
@@ -165,8 +166,8 @@
 
 
 def fused_kernel(
-    pieces, weight, grads, acts, product,
-    sides, low, head, left, right, tail, rays, raw, held_weight,
+    activations, out_grads, weight, grads, acts, product,
+    staged, f_sem, pieces, sides, low, head, left, right, tail, rays, raw, held_weight,
     z_send, send, recv, d_recv, c_send, c_recv, local, w_sem, r_send, r_recv,
     g_send, y_send, t_send, g_recv, y_recv, t_recv, a_send, a_recv, h_send, h_recv, k_send, k_recv, put,
 ):
@@ -218,7 +219,21 @@
         return remote(band(oi, s), band(oi, s), c_send.at[0], c_recv.at[n], c_peer)
 
     d_peer = {"tok": z, "out": ox, "grp": 1 - y}
-    greet(z_peers + [y_peer, x_peer, c_peer, d_peer])
+
+    def fetch(i, source):
+        return pltpu.make_async_copy(source, staged.at[i], f_sem.at[i])
+
+    fetch(0, activations).start()
+    fetch(1, out_grads).start()
+
+    def part_blocks():
+        for i, source in enumerate((activations, out_grads)):
+            fetch(i, source).wait()
+            value = staged[i]
+            for k in range(2):
+                pieces[2 * i + k] = value[:, k, :]
+
+    greet(z_peers + [y_peer, x_peer, c_peer, d_peer], part_blocks)
     strip = width // 2
     strips = [(b, i) for b in range(2) for i in range(2)]
 
@@ -622,12 +637,12 @@
     settle(sides.at[pl.ds(0, tokens // 2), :], c_send.at[0])
 
 
-def fused(pieces, weight, part):
-    _, rows, width = pieces.shape
+def fused(activations, out_grads, weight, part):
+    rows, _, width = activations.shape
     tokens, block = rows * 8, width * 4
     dma = pltpu.SemaphoreType.DMA
     vmem = pl.BlockSpec(memory_space=pltpu.VMEM)
-    low = pieces.dtype
+    low = activations.dtype
     return pl.pallas_call(
         fused_kernel,
         out_shape=(
@@ -635,9 +650,12 @@
             jax.ShapeDtypeStruct((tokens, 2 * part), low),
             jax.ShapeDtypeStruct((rows, 2, width), low),
         ),
-        in_specs=[vmem, pl.BlockSpec(memory_space=pltpu.HBM)],
+        in_specs=[pl.BlockSpec(memory_space=pltpu.HBM)] * 3,
         out_specs=(vmem, vmem, vmem),
         scratch_shapes=[
+            pltpu.VMEM((2, rows, 2, width), low),
+            dma((2,)),
+            pltpu.VMEM((4, rows, width), low),
             pltpu.VMEM((tokens, block), low),
             pltpu.VMEM((tokens, tokens), low),
             pltpu.VMEM((tokens, part), jnp.float32),
@@ -673,7 +691,11 @@
         ],
         compiler_params=pltpu.CompilerParams(collective_id=0, has_side_effects=True, vmem_limit_bytes=ROOM),
         name="fused",
-    )(pieces, weight)
+    )(
+        pltpu.with_memory_space_constraint(activations, pltpu.HBM),
+        pltpu.with_memory_space_constraint(out_grads, pltpu.HBM),
+        weight,
+    )
 
 
 def update_kernel(grads, acts, product, update, input_grad, sem):
@@ -727,8 +749,7 @@
     tok_dev, _, width = activations.shape
     part = width // lax.axis_size("grp")
     token_count = tok_dev * lax.axis_size(("tok", "grp"))
-    pieces = jnp.swapaxes(jnp.concatenate([activations, out_grads], axis=1), 0, 1)
-    grads_low, acts_low, product = fused(pieces, weight, part)
+    grads_low, acts_low, product = fused(activations, out_grads, weight, part)
     return update_product(grads_low, acts_low, product)
 
 

time: 64.9 us -> 62.9 us (0.969)
  local copies, waits for them, and re-layouts: 1.96 us -> 0 us
    unnamed x2 -> x0, local copies, waits for them, and re-layouts: 1.96 us -> none
where the time goes in v7:
time: 62.9 us; the launch traced here: 62.8 us
  Pallas kernels  62 us (99%)
  between operations  0.8 us (1%)
    pallas_call x1, Pallas kernels, fused(): pl.pallas_call(fused_kernel, out_shape=(jax.ShapeDtypeStruct((2, tokens,...  58.2 us
    pallas_call x1, Pallas kernels, update_product(): pl.pallas_call(update_kernel, grid=(STEPS,), out_shape=(jax.ShapeDtypeStr...  3.79 us

profile of v7, /device:TPU:0, one launch (start us, length us, event | category | flops | bytes accessed | tf_op | source)
XLA Modules:
  0.0 62.8 jit_solution(13411630233443283627)
XLA Ops:
  0.6 58.2 %fused.1 = (bf16[2,1024,512]{2,1,0:T(8,128)(2,1)S(1)}, bf16[1024,512]{1,0:T(8,128)(2,1)S(1)}, bf16[128,2,512]{2,1,0:T(2,128)(2,1)S(1)}) custom-call(bf16[128,2,512]{2,1,0:T(2,128)(2,1)} %activations.1, bf16[128,2,512]{2,1,0:T(2,128)(2,1)} %out_grads.1, bf16[2,512,4096]{2,1,0:T(8,128)(2,1)} %weight.1), custom_call_target="tpu_custom_call" | custom-call | tf_op jit(solution)/shard_map/fused/pallas_call | solution.py:646
  58.9 3.8 %update.1 = (bf16[512,2,512]{2,1,0:T(2,128)(2,1)}, bf16[128,2,512]{2,1,0:T(2,128)(2,1)}) custom-call(bf16[2,1024,512]{2,1,0:T(8,128)(2,1)S(1)} %get-tuple-element.5.grads, bf16[1024,512]{1,0:T(8,128)(2,1)S(1)} %get-tuple-element.6.acts, bf16[128,2,512]{2,1,0:T(2,128)(2,1)S(1)} %get-tuple-element.7.product), custom_call_target="tpu_custom_call" | custom-call | tf_op jit(solution)/shard_map/update/pallas_call | solution.py:730

commit v8 on v7

--- a/solution.py
+++ b/solution.py
@@ -118,7 +118,7 @@
 TURNED = 1
 CORNER = 3
 ROOM = 50 * 2**20
-STEPS = 2
+STEPS = 1
 PARTS = 4
 PLAN = (
     ("y", 0, 0), ("x", 0, 0), ("y", 0, 1), ("x", 0, 1), ("z", 1, 0), ("y", 0, 2), ("x", 0, 2),

time: 62.9 us -> 62.8 us (level)
  no operation moved by 1% of the time
where the time goes in v8:
time: 62.8 us; the launch traced here: 62.7 us
  Pallas kernels  61.9 us (99%)
  between operations  0.8 us (1%)
    pallas_call x1, Pallas kernels, fused(): pl.pallas_call(fused_kernel, out_shape=(jax.ShapeDtypeStruct((2, tokens,...  58.2 us
    pallas_call x1, Pallas kernels, update_product(): pl.pallas_call(update_kernel, grid=(STEPS,), out_shape=(jax.ShapeDtypeStr...  3.69 us

profile of v8, /device:TPU:0, one launch (start us, length us, event | category | flops | bytes accessed | tf_op | source)
XLA Modules:
  0.0 62.7 jit_solution(16525439603492174923)
XLA Ops:
  0.6 58.2 %fused.1 = (bf16[2,1024,512]{2,1,0:T(8,128)(2,1)S(1)}, bf16[1024,512]{1,0:T(8,128)(2,1)S(1)}, bf16[128,2,512]{2,1,0:T(2,128)(2,1)S(1)}) custom-call(bf16[128,2,512]{2,1,0:T(2,128)(2,1)} %activations.1, bf16[128,2,512]{2,1,0:T(2,128)(2,1)} %out_grads.1, bf16[2,512,4096]{2,1,0:T(8,128)(2,1)} %weight.1), custom_call_target="tpu_custom_call" | custom-call | tf_op jit(solution)/shard_map/fused/pallas_call | solution.py:646
  58.9 3.7 %update.1 = (bf16[512,2,512]{2,1,0:T(2,128)(2,1)}, bf16[128,2,512]{2,1,0:T(2,128)(2,1)}) custom-call(bf16[2,1024,512]{2,1,0:T(8,128)(2,1)S(1)} %get-tuple-element.5.grads, bf16[1024,512]{1,0:T(8,128)(2,1)S(1)} %get-tuple-element.6.acts, bf16[128,2,512]{2,1,0:T(2,128)(2,1)S(1)} %get-tuple-element.7.product), custom_call_target="tpu_custom_call" | custom-call | tf_op jit(solution)/shard_map/update/pallas_call | solution.py:730
